TPU v7x, 32 devices: a whole 2x2x4 slice. The times are simulated.
32 devices in a mesh: group: 2 (over x), seq: 16 (over z, y, core).
Axes of the slice: x: 2, y: 2, z: 4, core: 2. Of those that a mesh axis runs over, the one named last changes fastest.
Arguments:
- tokens: bfloat16 [16384, 4096], P(('group', 'seq')), parts along dimension 0, may hold values from -6 to 6
- norm_gain: bfloat16 [4096], replicated, may hold values from 0.099609375 to 1.8984375
- w_key: bfloat16 [4096, 1024], P('seq'), may hold values from -0.09375 to 0.09375
- w_value: bfloat16 [4096, 1024], P('seq'), may hold values from -0.09375 to 0.09375
- lengths: int32 [4], P('group'), parts along dimension 0, may hold values from 2048 to 4096
- page_table: int32 [1024], P(('group', 'seq')), parts along dimension 0, may hold values from 0 to 639, as said below
Outputs:
- kv_cache: bfloat16 [2, 1280, 16, 1024], P(None, ('group', 'seq')), parts along dimension 1
There are 2 independent parts, one for each index of `group`. A program takes and returns all parts, laid end to end along the dimension named above; an argument that names none is the same for every part. Nothing has to cross between parts.
Inputs may be any that keep to these rules, and one draw needn't show every extreme that they name: The entries are distinct. Page g of the 32 pages of device s goes to slot page_table[g] of decode device page_table[g] // 40, which is s + k modulo 16 for an offset k in -2 .. 2, at a slot of the block of 8 slots from (k + 2) * 8 on; so at most 8 pages go from one device to one decode device, and exactly 8 from every device to some decode device.
All inputs are finite; a program needn't handle non-finite values.
Results may differ from a plain program's by a relative error of at most 0.0049.
Values may be sent and summed in bfloat16 or wider, within the bound.
A program may use at most 64 MiB of HBM per device.

v0:
```python
import functools

import jax
import jax.numpy as jnp
import numpy as np
from jax import lax
from jax.experimental import pallas as pl
from jax.experimental.pallas import tpu as pltpu
from jax.sharding import PartitionSpec as P

HEAD = 128
PAGE = 16
REACH = 2
CAP = 8
SLOTS = 40
REGIONS = 2 * REACH + 1
BLOCK = CAP * PAGE
ROWS = SLOTS * PAGE

ROPE_THETA = 500000.0
EPS = 1e-05

CHUNKS = 8
TILE = 256
WAVE = 8
LAG = 2
MIXED = (0, 2, 4)
MESH = pl.DeviceIdType.MESH


def kernel(
    n, tokens, gain, w_key, w_value, lengths, pages, freq, out,
    wbuf, xbuf, pbuf, onehot, cosine, sine,
    load_sem, tok_sem, ys, yr, fr, zs, zr, xs, xr, cs, cr, hs, hr,
):
    chunks, depth = wbuf.shape[0], wbuf.shape[1]
    half, width = wbuf.shape[5], wbuf.shape[6]
    per_kind = chunks // 2
    tok_rows, features = xbuf.shape
    group = lax.axis_index("group")
    me = lax.axis_index("seq")
    core, y, z = lax.rem(me, 2), lax.rem(me // 2, 2), me // 4
    other_core, other_y, other_group = 1 - core, 1 - y, 1 - group

    def seq_of(z_at, y_at, core_at):
        return (z_at * 2 + y_at) * 2 + core_at

    def piece(j, z_at, y_at, part):
        return wbuf.at[j, z_at, y_at, core, part]

    def send(ref, send_sem, recv_sem, group_at, seq_at, dst=None):
        pltpu.make_async_remote_copy(
            src_ref=ref,
            dst_ref=ref if dst is None else dst,
            send_sem=send_sem,
            recv_sem=recv_sem,
            device_id={"group": group_at, "seq": seq_at},
            device_id_type=MESH,
        ).start()

    def wait(ref, sem):
        pltpu.make_async_copy(ref, ref, sem).wait()

    loads = []
    for j in range(chunks):
        w_ref = w_key if j < per_kind else w_value
        columns = pl.ds((j % per_kind) * width, width)
        for part in range(2):
            copy = pltpu.make_async_copy(
                w_ref.at[pl.ds(part * half, half), columns],
                wbuf.at[j, z, y, core, part],
                load_sem.at[j, part],
            )
            copy.start()
            loads.append(copy)
    token_copy = pltpu.make_async_copy(tokens, xbuf, tok_sem)
    token_copy.start()

    to_y = seq_of(z, other_y, core)
    to_core = seq_of(z, y, other_core)
    has_up, has_down = z + 1 < depth, z > 0
    up = seq_of(lax.rem(z + 1, depth), y, core)
    down = seq_of(lax.rem(z + depth - 1, depth), y, core)

    barrier = pltpu.get_barrier_semaphore()

    def greet(group_at, seq_at):
        pl.semaphore_signal(
            barrier, inc=1, device_id={"group": group_at, "seq": seq_at}, device_id_type=MESH
        )

    greet(group, up)
    greet(group, down)
    greet(group, to_y)
    greet(group, to_core)
    greet(other_group, me)
    for region in range(REGIONS):
        if region != REACH:
            greet(group, lax.rem(me + region - REACH + n, n))
    pl.semaphore_wait(barrier, 5 + REGIONS - 1)

    def to_partner(j, ref):
        send(ref, cs.at[j], cr.at[j], group, to_core)

    def go_up(j, z_at, y_at, k):
        @pl.when(has_up)
        def _():
            send(piece(j, z_at, y_at, group), zs.at[j, 0, k], zr.at[j, y_at, z_at], group, up)

    def go_down(j, z_at, y_at, k):
        @pl.when(has_down)
        def _():
            send(piece(j, z_at, y_at, group), zs.at[j, 1, k], zr.at[j, y_at, z_at], group, down)

    def begin(j):
        for part in (0, 1):
            ref = piece(j, z, y, part)
            send(ref, ys.at[j], yr.at[j, part], group, to_y)
        go_up(j, z, y, 0)
        go_down(j, z, y, 0)
        for part in (0, 1):
            to_partner(j, piece(j, z, y, part))

    def cross(j):
        for part in (0, 1):
            wait(piece(j, z, other_y, part), yr.at[j, part])
        if j not in MIXED:
            go_up(j, z, other_y, 0)
            go_down(j, z, other_y, 0)
        for part in (0, 1):
            to_partner(j, piece(j, z, other_y, part))

    def arrive(j, z_at, y_at):
        ref = piece(j, z_at, y_at, group)
        wait(ref, zr.at[j, y_at, z_at])
        return ref

    def pass_on(j, ref, z_at, y_at):
        send(ref, xs.at[j], xr.at[j, y_at, z_at], other_group, me)
        to_partner(j, ref)
        if j in MIXED:
            send(ref, ys.at[j], fr.at[j, 0, z_at], group, to_y)

    def lines(j):
        return (y,) if j in MIXED else (y, other_y)

    def along(j, k):
        for y_at in lines(j):
            @pl.when(z - k >= 0)
            def _():
                ref = arrive(j, z - k, y_at)
                go_up(j, z - k, y_at, k)
                pass_on(j, ref, z - k, y_at)

            @pl.when(z + k < depth)
            def _():
                ref = arrive(j, z + k, y_at)
                go_down(j, z + k, y_at, k)
                pass_on(j, ref, z + k, y_at)

    def others(visit):
        def body(k, carry):
            @pl.when(z - k >= 0)
            def _():
                visit(z - k)

            @pl.when(z + k < depth)
            def _():
                visit(z + k)

            return carry

        lax.fori_loop(1, depth, body, 0)

    def finish(j):
        def visit(zz):
            for y_at in lines(j):
                ref = piece(j, zz, y_at, other_group)
                wait(ref, xr.at[j, y_at, zz])
                if j in MIXED:
                    send(ref, ys.at[j], fr.at[j, 1, zz], group, to_y)
                to_partner(j, ref)
            if j in MIXED:
                ref = piece(j, zz, other_y, group)
                wait(ref, fr.at[j, 0, zz])
                to_partner(j, ref)

        others(visit)

    def settle(j):
        def visit(zz):
            ref = piece(j, zz, other_y, other_group)
            wait(ref, fr.at[j, 1, zz])
            to_partner(j, ref)

        if j in MIXED:
            others(visit)

    length_each = tok_rows * n // 2
    first = lax.rem(me * tok_rows, length_each)

    def normalise(at, rows_here):
        def body(i, carry):
            rows = pl.ds(pl.multiple_of(at + i * 32, 32), 32)
            wide = xbuf[rows, :].astype(jnp.float32)
            scale = lax.rsqrt(jnp.mean(wide * wide, axis=1, keepdims=True) + EPS)
            xbuf[rows, :] = (wide * scale * gain[...].astype(jnp.float32)).astype(jnp.bfloat16)
            return carry

        lax.fori_loop(0, rows_here // 32, body, 0)

    def mark_rows():
        second_prompt = (me * tok_rows) // length_each
        limit = lengths[0] + second_prompt * (lengths[1] - lengths[0])
        page_count = tok_rows // PAGE
        token = lax.broadcasted_iota(jnp.int32, (page_count, tok_rows), 1)
        page = lax.broadcasted_iota(jnp.int32, (page_count, tok_rows), 0)
        used = jnp.where((token // PAGE == page) & (first + token < limit), 1.0, 0.0)
        used = used.astype(jnp.bfloat16)
        slot = lax.rem(pages[...], SLOTS)

        def hot(i, carry):
            at = i * BLOCK
            row = lax.broadcasted_iota(jnp.int32, (BLOCK, page_count), 0) + at
            held = jnp.where(row // PAGE == slot, 1.0, 0.0).astype(jnp.bfloat16)
            spread = jnp.dot(held, used, preferred_element_type=jnp.float32)
            row = lax.broadcasted_iota(jnp.int32, (BLOCK, tok_rows), 0)
            column = lax.broadcasted_iota(jnp.int32, (BLOCK, tok_rows), 1)
            same = lax.rem(row, PAGE) == lax.rem(column, PAGE)
            onehot[pl.ds(pl.multiple_of(at, BLOCK), BLOCK), :] = jnp.where(
                same, spread, 0.0
            ).astype(jnp.bfloat16)
            return carry

        lax.fori_loop(0, REGIONS, hot, 0)

    def angles():
        def turn(i, carry):
            at = pl.multiple_of(i * 64, 64)
            row = lax.broadcasted_iota(jnp.int32, (64, HEAD), 0) + (first + at)
            lane = lax.broadcasted_iota(jnp.int32, (64, HEAD), 1)
            angle = row.astype(jnp.float32) * freq[...]
            cosine[pl.ds(at, 64), :] = jnp.cos(angle)
            sined = jnp.sin(angle)
            sine[pl.ds(at, 64), :] = jnp.where(lane < HEAD // 2, -sined, sined)
            return carry

        lax.fori_loop(0, tok_rows // 64, turn, 0)

    def project(j):
        wait(wbuf.at[j, :, :, other_core], cr.at[j])
        for t in range(width // TILE):
            at = t * TILE
            weights = wbuf[j, :, :, :, :, :, at : at + TILE].reshape(features, TILE)
            raw = jnp.dot(xbuf[...], weights, preferred_element_type=jnp.float32)
            if j < per_kind:
                heads = []
                for head in range(TILE // HEAD):
                    one = raw[:, head * HEAD : (head + 1) * HEAD]
                    heads.append(
                        one * cosine[...] + pltpu.roll(one, HEAD // 2, 1) * sine[...]
                    )
                raw = jnp.concatenate(heads, axis=1)
            placed = jnp.dot(
                onehot[...], raw.astype(jnp.bfloat16), preferred_element_type=jnp.float32
            )
            pbuf[j, :, at : at + TILE] = placed.astype(jnp.bfloat16)

    def spot(j, region):
        rows = pl.ds(region * BLOCK, BLOCK)
        return (
            pbuf.at[j, rows, :],
            out.at[j // per_kind, rows, pl.ds((j % per_kind) * width, width)],
        )

    def hand_over(j):
        for region in (0, 4, 1, 3, 2):
            src, dst = spot(j, region)
            if region == REACH:
                pltpu.make_async_copy(src, dst, hr.at[j, region]).start()
            else:
                send(src, hs.at[j, region], hr.at[j, region], group,
                     lax.rem(me + region - REACH + n, n), dst)

    def stage(j, k):
        if k == 0:
            cross(j)
        else:
            along(j, k)

    for j in range(chunks):
        for copy in loads[2 * j : 2 * j + 2]:
            copy.wait()
        begin(j)
    quarter = tok_rows // 4
    jobs = [token_copy.wait]
    jobs += [functools.partial(normalise, i * quarter, quarter) for i in range(4)]
    jobs += [mark_rows, angles]
    if depth <= WAVE:
        for t in range(chunks + depth + LAG):
            for j in range(chunks):
                k = t - j
                if 0 <= k < depth:
                    stage(j, k)
            for job in jobs[2 * t : 2 * t + 2]:
                job()
            if 0 <= t - depth < chunks:
                finish(t - depth)
            if 0 <= t - depth - 1 < chunks:
                settle(t - depth - 1)
            if 0 <= t - depth - LAG < chunks:
                project(t - depth - LAG)
                hand_over(t - depth - LAG)
    else:
        for job in jobs:
            job()
        for j in range(chunks):
            stage(j, 0)
            lax.fori_loop(1, depth, lambda k, carry: (along(j, k), carry)[1], 0)
            finish(j)
            settle(j)
            project(j)
            hand_over(j)

    for j in range(chunks):
        if j in MIXED:
            wait(wbuf.at[j, :, y, core], ys.at[j])
            wait(wbuf.at[j, 1:, y, core, group], xs.at[j])
        else:
            wait(wbuf.at[j, z, y, core], ys.at[j])
            wait(wbuf.at[j, 1:, :, core, group], xs.at[j])
        sent = wbuf.at[j, 0, :, core, group]
        if j in MIXED:
            sent = wbuf.at[j, 0, y, core, group]
        wait(wbuf.at[j, :, :, core], cs.at[j])

        def drain(k, carry):
            @pl.when(has_up & (z - k >= 0))
            def _():
                wait(sent, zs.at[j, 0, k])

            @pl.when(has_down & (z + k < depth))
            def _():
                wait(sent, zs.at[j, 1, k])

            return carry

        lax.fori_loop(0, depth, drain, 0)
        for region in range(REGIONS):
            src, dst = spot(j, region)
            wait(dst, hr.at[j, region])
            if region != REACH:
                wait(src, hs.at[j, region])


def on_device(n, tokens, norm_gain, w_key, w_value, lengths, page_table):
    tok_rows, features = tokens.shape
    columns = w_key.shape[1]
    freq = ROPE_THETA ** (-(np.arange(HEAD // 2) * 2.0 / HEAD))
    freq = np.concatenate([freq, freq]).astype(np.float32)[None, :]
    depth = n // 4
    half = w_key.shape[0] // 2
    width = 2 * columns // CHUNKS
    dma = pltpu.SemaphoreType.DMA
    vmem = pl.BlockSpec(memory_space=pltpu.VMEM)
    smem = pl.BlockSpec(memory_space=pltpu.SMEM)
    hbm = pl.BlockSpec(memory_space=pl.ANY)
    cache = pl.pallas_call(
        functools.partial(kernel, n),
        out_shape=jax.ShapeDtypeStruct((2, ROWS, columns), jnp.bfloat16),
        in_specs=[hbm, vmem, hbm, hbm, smem, vmem, vmem],
        out_specs=hbm,
        scratch_shapes=[
            pltpu.VMEM((CHUNKS, depth, 2, 2, 2, half, width), jnp.bfloat16),
            pltpu.VMEM((tok_rows, features), jnp.bfloat16),
            pltpu.VMEM((CHUNKS, ROWS, width), jnp.bfloat16),
            pltpu.VMEM((ROWS, tok_rows), jnp.bfloat16),
            pltpu.VMEM((tok_rows, HEAD), jnp.float32),
            pltpu.VMEM((tok_rows, HEAD), jnp.float32),
            dma((CHUNKS, 2)),
            dma,
            dma((CHUNKS,)), dma((CHUNKS, 2)), dma((CHUNKS, 2, depth)),
            dma((CHUNKS, 2, depth)), dma((CHUNKS, 2, depth)),
            dma((CHUNKS,)), dma((CHUNKS, 2, depth)),
            dma((CHUNKS,)), dma((CHUNKS,)),
            dma((CHUNKS, REGIONS)), dma((CHUNKS, REGIONS)),
        ],
        compiler_params=pltpu.CompilerParams(
            collective_id=0, has_side_effects=True, vmem_limit_bytes=60 * 2**20
        ),
    )(tokens, norm_gain[None, :], w_key, w_value, lengths, page_table[None, :], freq)
    return cache.reshape(2, SLOTS, PAGE, columns)


def solution(mesh):
    placed = (
        P(("group", "seq"), None),
        P(),
        P("seq", None),
        P("seq", None),
        P("group"),
        P(("group", "seq")),
    )
    return jax.shard_map(
        functools.partial(on_device, mesh.shape["seq"]),
        mesh=mesh,
        in_specs=placed,
        out_specs=P(None, ("group", "seq"), None, None),
        check_vma=False,
    )
```

profile of v0, /device:TPU:1, one launch (start us, length us, event | category | flops | bytes accessed | tf_op | source)
XLA Modules:
  0.0 101.1 jit_solution(2001759398667523018)
XLA Ops:
  0.0 1.3 %broadcast_in_dim.6.gain = bf16[1,4096]{1,0:T(2,128)(2,1)} reshape(bf16[4096]{0:T(1024)(128)(2,1)} %param.8) | data formatting | bytes 16384 | tf_op jit(solution)/shard_map/broadcast_in_dim | solution.py:391
  1.3 96.1 %shard_map.73 = bf16[2,640,1024]{2,1,0:T(8,128)(2,1)} custom-call(bf16[512,4096]{1,0:T(8,128)(2,1)} %tokens.1, bf16[1,4096]{1,0:T(2,128)(2,1)} %broadcast_in_dim.6.gain, bf16[256,1024]{1,0:T(8,128)(2,1)} %w_key.1, bf16[256,1024]{1,0:T(8,128)(2,1)} %w_value.1, s32[2]{0:T(128)} %lengths.1, s32[1,32]{1,0:T(1,128)} %bitcast.3, f32[1,128]{1,0:T(1,128)} %constant.2.clone.freq), custom_call_target="tpu_custom_call" | custom-call | tf_op jit(solution)/shard_map/pallas_call | solution.py:368
  97.5 3.7 %copy.9 = bf16[2,40,16,1024]{3,2,1,0:T(8,128)(2,1)} copy(bf16[2,40,16,1024]{3,2,1,0:T(8,128)(2,1)} %bitcast.2) | data formatting | bytes 5242880
where the time goes:
time: 101 us
  Pallas kernels  96.1 us (95%)
  local copies, waits for them, and re-layouts  4.98 us (5%)
    pallas_call x1, Pallas kernels, on_device(): pl.pallas_call(functools.partial(kernel, n), out_shape=jax.ShapeDtypeStru...  96.1 us
    unnamed x1, local copies, waits for them, and re-layouts  3.67 us

commit v1 on v0

v1 whole, which is shorter than its diff:
```python
import functools

import jax
import jax.numpy as jnp
import numpy as np
from jax import lax
from jax.experimental import pallas as pl
from jax.experimental.pallas import tpu as pltpu
from jax.sharding import PartitionSpec as P

HEAD = 128
PAGE = 16
REACH = 2
CAP = 8
SLOTS = 40
REGIONS = 2 * REACH + 1
BLOCK = CAP * PAGE
ROWS = SLOTS * PAGE

ROPE_THETA = 500000.0
EPS = 1e-05

TILE = 256
MESH = pl.DeviceIdType.MESH

PAIRED, SPLIT, TURNED = 0, 1, 2
CHUNKS = ((SPLIT, True), (PAIRED, False), (PAIRED, True), (SPLIT, True), (PAIRED, True), (SPLIT, True), (PAIRED, True), (PAIRED, True))
GROUPS = (1, 1, 1, 1, 1, 1, 1, 1)
RELAYED = (1, 5)

LAYERS = 4
LOOP_CHUNKS = 8

BEGIN, CROSS, ACROSS, ALONG, FACE, SIDE, SETTLE, UP, DOWN, RELAY = range(10)
COMPUTE = (0,0,0,0,0,0,0,0,0,0,0,0,0,0,0,0,0,0,0,0,1,1,1,1,1,1,1,1)
END = (
    ((BEGIN, 0, 0, 0), (BEGIN, 0, 0, 1), (BEGIN, 1, 0, 0), (BEGIN, 1, 0, 1), (BEGIN, 2, 0, 0),),
    (),
    (),
    (),
    (),
    (),
    ((BEGIN, 2, 0, 1),),
    (),
    ((BEGIN, 3, 0, 0), (ALONG, 0, 1, -1), (ALONG, 0, 1, 0), (ALONG, 0, 1, 1),),
    ((CROSS, 0, 0, -1), (CROSS, 0, 0, 0), (CROSS, 0, 0, 1),),
    (),
    (),
    ((CROSS, 1, 0, -1), (CROSS, 1, 0, 0), (CROSS, 1, 0, 1),),
    (),
    ((FACE, 0, 1, -1), (FACE, 0, 1, 0),),
    ((BEGIN, 3, 0, 1), (ALONG, 3, 1, -1), (ALONG, 3, 1, 0),),
    ((BEGIN, 4, 0, 0),),
    ((ALONG, 3, 1, 1), (CROSS, 2, 0, -1), (CROSS, 2, 0, 1),),
    ((CROSS, 2, 0, 0), (ALONG, 1, 1, -1), (ALONG, 1, 1, 0),),
    ((ACROSS, 1, 0, -1), (ACROSS, 1, 0, 0), (ACROSS, 1, 0, 1),),
    ((BEGIN, 4, 0, 1), (ALONG, 2, 1, -1), (ALONG, 2, 1, 0), (FACE, 3, 1, -1), (FACE, 3, 1, 0), (SETTLE, 0, 1, -1),
     (SETTLE, 0, 1, 0), (BEGIN, 5, 0, 0), (ALONG, 0, 2, -1), (ALONG, 0, 2, 0), (ALONG, 0, 2, 1),
     (BEGIN, 5, 0, 1), (CROSS, 3, 0, -1), (CROSS, 3, 0, 1), (FACE, 1, 1, -1), (FACE, 1, 1, 0), (ALONG, 1, 2, -1),
     (ALONG, 1, 2, 0), (CROSS, 3, 0, 0), (BEGIN, 6, 0, 0), (FACE, 0, 2, -1), (FACE, 0, 2, 0), (BEGIN, 7, 0, 0),
     (BEGIN, 6, 0, 1), (ALONG, 2, 2, -1), (ALONG, 2, 2, 0), (SETTLE, 3, 1, -1), (SETTLE, 3, 1, 0),
     (FACE, 2, 1, -1), (FACE, 2, 1, 0), (ALONG, 3, 2, -1), (ALONG, 3, 2, 0), (ALONG, 3, 2, 1), (SETTLE, 0, 2, -1),
     (SETTLE, 0, 2, 0), (BEGIN, 7, 0, 1), (ALONG, 0, 3, -1), (ALONG, 0, 3, 0), (ALONG, 0, 3, 1),
     (FACE, 1, 2, -1), (FACE, 1, 2, 0), (CROSS, 4, 0, -1), (CROSS, 4, 0, 0), (CROSS, 4, 0, 1), (ALONG, 4, 1, -1),
     (ALONG, 4, 1, 0), (FACE, 2, 2, -1), (FACE, 2, 2, 0), (FACE, 0, 3, -1), (FACE, 0, 3, 0), (ALONG, 4, 2, -1),
     (ALONG, 4, 2, 0), (FACE, 3, 2, -1), (FACE, 3, 2, 0), (CROSS, 5, 0, -1), (CROSS, 5, 0, 0), (CROSS, 5, 0, 1),
     (ALONG, 1, 3, -1), (ALONG, 1, 3, 0), (SETTLE, 0, 3, -1), (SETTLE, 0, 3, 0), (FACE, 4, 1, -1),
     (FACE, 4, 1, 0), (SETTLE, 3, 2, -1), (SETTLE, 3, 2, 0), (ALONG, 2, 3, -1), (ALONG, 2, 3, 0),
     ),
    ((FACE, 4, 2, -1), (FACE, 4, 2, 0), (ALONG, 5, 1, -1), (ALONG, 5, 1, 0), (ALONG, 5, 1, 1), (CROSS, 6, 0, -1),
     (CROSS, 6, 0, 0), (CROSS, 6, 0, 1), (ALONG, 5, 2, -1), (ALONG, 5, 2, 0), (ALONG, 5, 2, 1),
     (FACE, 1, 3, -1), (FACE, 1, 3, 0), (ALONG, 3, 3, -1), (ALONG, 3, 3, 0), (ALONG, 3, 3, 1), (CROSS, 7, 0, -1),
     (CROSS, 7, 0, 1), (DOWN, 0, 0, 0), (UP, 0, 0, 0), (CROSS, 7, 0, 0),),
    ((FACE, 2, 3, -1), (FACE, 2, 3, 0), (ALONG, 6, 1, -1), (ALONG, 6, 1, 0), (FACE, 3, 3, -1), (FACE, 3, 3, 0),
     (FACE, 5, 1, -1), (FACE, 5, 1, 0), (DOWN, 1, 0, 0), (UP, 1, 0, 0),),
    ((ALONG, 6, 2, -1), (ALONG, 6, 2, 0), (FACE, 5, 2, -1), (FACE, 5, 2, 0), (SETTLE, 3, 3, -1),
     (SETTLE, 3, 3, 0), (DOWN, 2, 0, 0), (UP, 2, 0, 0), (ALONG, 4, 3, -1), (ALONG, 4, 3, 0), (SETTLE, 5, 1, -1),
     (SETTLE, 5, 1, 0), (FACE, 6, 1, -1), (FACE, 6, 1, 0), (ALONG, 5, 3, -1), (ALONG, 5, 3, 0),
     (ALONG, 5, 3, 1),),
    ((DOWN, 3, 0, 0), (UP, 3, 0, 0), (SETTLE, 5, 2, -1), (SETTLE, 5, 2, 0), (FACE, 6, 2, -1), (FACE, 6, 2, 0),
     (ALONG, 7, 1, -1), (ALONG, 7, 1, 0), (FACE, 4, 3, -1), (FACE, 4, 3, 0), (ALONG, 7, 2, -1),
     (ALONG, 7, 2, 0), (FACE, 5, 3, -1), (FACE, 5, 3, 0),),
    ((DOWN, 4, 0, 0), (UP, 4, 0, 0), (FACE, 7, 1, -1), (FACE, 7, 1, 0), (ALONG, 6, 3, -1), (ALONG, 6, 3, 0),
     (SETTLE, 5, 3, -1), (SETTLE, 5, 3, 0), (FACE, 7, 2, -1), (FACE, 7, 2, 0),),
    ((DOWN, 5, 0, 0), (UP, 5, 0, 0), (FACE, 6, 3, -1), (FACE, 6, 3, 0), (ALONG, 7, 3, -1), (ALONG, 7, 3, 0),
     ),
    ((DOWN, 6, 0, 0), (UP, 6, 0, 0), (FACE, 7, 3, -1), (FACE, 7, 3, 0),),
    ((DOWN, 7, 0, 0), (UP, 7, 0, 0),),
)
INNER = (
    ((BEGIN, 0, 0, 0), (BEGIN, 0, 0, 1), (BEGIN, 0, 0, 2), (BEGIN, 1, 0, 0), (BEGIN, 1, 0, 1), (BEGIN, 1, 0, 2),
     (BEGIN, 2, 0, 0), (BEGIN, 2, 0, 1), (BEGIN, 2, 0, 2),),
    (),
    (),
    ((BEGIN, 3, 0, 0),),
    ((BEGIN, 3, 0, 1),),
    ((BEGIN, 4, 0, 0),),
    (),
    ((CROSS, 0, 0, -1), (CROSS, 0, 0, 0), (CROSS, 0, 0, 1), (BEGIN, 5, 0, 0), (BEGIN, 3, 0, 2),
     ),
    (),
    ((BEGIN, 6, 0, 0), (CROSS, 1, 0, -1), (CROSS, 1, 0, 0), (CROSS, 1, 0, 1), (CROSS, 1, 0, 2),
     ),
    ((BEGIN, 7, 0, 0),),
    ((CROSS, 2, 0, -1), (CROSS, 2, 0, 0), (CROSS, 2, 0, 1), (CROSS, 2, 0, 2),),
    ((BEGIN, 4, 0, 2),),
    ((ACROSS, 0, 0, -1), (ACROSS, 0, 0, 0), (CROSS, 3, 0, -1), (CROSS, 3, 0, 0), (CROSS, 3, 0, 1),
     ),
    ((ALONG, 0, 2, -1), (ALONG, 0, 2, 0), (ALONG, 0, 2, 1),),
    ((ACROSS, 1, 0, -1), (ACROSS, 1, 0, 0), (BEGIN, 4, 0, 1),),
    ((CROSS, 4, 0, -1),),
    ((ALONG, 1, 2, -1), (ALONG, 1, 2, 0), (ALONG, 1, 2, 1),),
    ((ACROSS, 2, 0, -1), (ACROSS, 2, 0, 0), (CROSS, 5, 0, -1),),
    ((CROSS, 4, 0, 0), (ALONG, 0, 0, -1), (ALONG, 0, 0, 0), (ALONG, 0, 0, 1), (ALONG, 2, 2, -1),
     (ALONG, 2, 2, 0), (ALONG, 2, 2, 1),),
    ((BEGIN, 5, 0, 2), (ACROSS, 3, 0, -1), (ACROSS, 3, 0, 0), (CROSS, 6, 0, -1), (CROSS, 7, 0, -1),
     (BEGIN, 6, 0, 2), (ALONG, 3, 2, -1), (ALONG, 3, 2, 0), (FACE, 0, 2, -1), (FACE, 0, 2, 0), (CROSS, 4, 0, 1),
     (BEGIN, 5, 0, 1), (ALONG, 3, 2, 1), (BEGIN, 7, 0, 2), (ALONG, 1, 0, -1), (ALONG, 1, 0, 0),
     (ALONG, 1, 0, 1), (ALONG, 0, 3, -1), (ALONG, 0, 3, 0), (ALONG, 0, 3, 1), (FACE, 1, 2, -1),
     (FACE, 1, 2, 0), (BEGIN, 6, 0, 1), (ALONG, 2, 0, -1), (ALONG, 2, 0, 0), (ALONG, 2, 0, 1), (CROSS, 5, 0, 0),
     (ALONG, 4, 2, -1), (ALONG, 4, 2, 0), (FACE, 2, 2, -1), (FACE, 2, 2, 0), (CROSS, 4, 0, 2), (ALONG, 1, 3, -1),
     (ALONG, 1, 3, 0), (ALONG, 1, 3, 1), (FACE, 0, 3, -1), (FACE, 0, 3, 0), (BEGIN, 7, 0, 1),),
    ((CROSS, 6, 0, 0), (ALONG, 4, 2, 1), (ALONG, 3, 0, -1), (ALONG, 3, 0, 0), (ALONG, 3, 0, 1),
     (ALONG, 2, 3, -1), (ALONG, 2, 3, 0), (ALONG, 2, 3, 1), (FACE, 3, 2, -1), (FACE, 3, 2, 0), (ALONG, 5, 2, -1),
     (ALONG, 5, 2, 0), (FACE, 1, 3, -1), (FACE, 1, 3, 0), (ACROSS, 4, 0, -1), (ACROSS, 4, 0, 0),
     ),
    ((UP, 1, 0, 0), (DOWN, 1, 0, 0), (CROSS, 6, 0, 1), (CROSS, 7, 0, 0), (CROSS, 5, 0, 1), (UP, 0, 0, 0),
     (DOWN, 0, 0, 0), (ALONG, 4, 0, -1), (ALONG, 4, 0, 0), (ALONG, 4, 0, 1), (ALONG, 3, 3, -1),
     (ALONG, 3, 3, 0), (ALONG, 3, 3, 1), (FACE, 2, 3, -1), (FACE, 2, 3, 0), (ALONG, 5, 2, 1), (ALONG, 6, 2, -1),
     (ALONG, 6, 2, 0),),
    ((FACE, 4, 2, -1), (FACE, 4, 2, 0), (ALONG, 5, 0, -1), (ALONG, 5, 0, 0), (ALONG, 5, 0, 1), (ALONG, 4, 3, -1),
     (ALONG, 4, 3, 0), (ALONG, 4, 3, 1), (FACE, 3, 3, -1), (FACE, 3, 3, 0), (ALONG, 7, 2, -1), (UP, 2, 0, 0),
     (DOWN, 2, 0, 0), (ACROSS, 5, 0, -1), (ACROSS, 5, 0, 0), (CROSS, 7, 0, 1),),
    ((CROSS, 6, 0, 2), (ALONG, 7, 2, 0), (ALONG, 6, 0, -1), (ALONG, 6, 0, 0), (ALONG, 6, 0, 1),
     (ALONG, 5, 3, -1), (ALONG, 5, 3, 0), (ALONG, 5, 3, 1), (ALONG, 6, 2, 1), (FACE, 5, 2, -1),
     (FACE, 5, 2, 0), (UP, 3, 0, 0), (DOWN, 3, 0, 0), (FACE, 4, 3, -1), (FACE, 4, 3, 0),),
    ((CROSS, 7, 0, 2), (ALONG, 6, 3, -1), (ALONG, 6, 3, 0), (ALONG, 6, 3, 1), (RELAY, 1, 0, 0),
     (UP, 4, 0, 0), (DOWN, 4, 0, 0), (ALONG, 7, 0, -1), (ALONG, 7, 0, 0), (ALONG, 7, 0, 1), (FACE, 5, 3, -1),
     (FACE, 5, 3, 0), (ACROSS, 6, 0, -1), (ACROSS, 6, 0, 0), (ALONG, 7, 2, 1),),
    ((DOWN, 5, 0, 0), (UP, 5, 0, 0), (FACE, 6, 2, -1), (FACE, 6, 2, 0), (FACE, 6, 3, -1), (FACE, 6, 3, 0),
     (ALONG, 7, 3, -1), (ALONG, 7, 3, 0), (ALONG, 7, 3, 1), (ACROSS, 7, 0, -1), (ACROSS, 7, 0, 0),
     ),
    ((DOWN, 6, 0, 0), (UP, 6, 0, 0), (FACE, 7, 2, -1), (FACE, 7, 2, 0), (FACE, 7, 3, -1), (FACE, 7, 3, 0),
     ),
    ((DOWN, 7, 0, 0), (UP, 7, 0, 0), (RELAY, 5, 0, 0),),
)


class Work:
    def __init__(self, n, refs, me):
        (self.gain, self.lengths, self.pages, self.freq, self.wide_gain, self.xbuf, self.onehot,
         self.cosine, self.sine) = refs
        self.n, self.me = n, me
        self.tok_rows, self.features = self.xbuf.shape
        self.length_each = self.tok_rows * n // 2
        self.first = lax.rem(me * self.tok_rows, self.length_each)

    def spread_gain(self):
        each = self.gain[...].astype(jnp.float32)
        rows = [each[i : i + 1, :] for i in range(self.features // HEAD)]
        self.wide_gain[...] = jnp.concatenate(rows, axis=1)

    def normalise(self, at, rows_here):
        xbuf = self.xbuf

        def body(i, carry):
            rows = pl.ds(pl.multiple_of(at + i * 32, 32), 32)
            wide = xbuf[rows, :].astype(jnp.float32)
            scale = lax.rsqrt(jnp.mean(wide * wide, axis=1, keepdims=True) + EPS)
            xbuf[rows, :] = (wide * scale * self.wide_gain[...]).astype(jnp.bfloat16)
            return carry

        lax.fori_loop(0, rows_here // 32, body, 0)

    def mark_rows(self):
        tok_rows = self.tok_rows
        second_prompt = (self.me * tok_rows) // self.length_each
        limit = self.lengths[0] + second_prompt * (self.lengths[1] - self.lengths[0])
        page_count = tok_rows // PAGE
        token = lax.broadcasted_iota(jnp.int32, (page_count, tok_rows), 1)
        page = lax.broadcasted_iota(jnp.int32, (page_count, tok_rows), 0)
        used = jnp.where((token // PAGE == page) & (self.first + token < limit), 1.0, 0.0)
        used = used.astype(jnp.bfloat16)
        slot = lax.rem(self.pages[...], SLOTS)

        def hot(i, carry):
            at = i * BLOCK
            row = lax.broadcasted_iota(jnp.int32, (BLOCK, page_count), 0) + at
            held = jnp.where(row // PAGE == slot, 1.0, 0.0).astype(jnp.bfloat16)
            spread = jnp.dot(held, used, preferred_element_type=jnp.float32)
            row = lax.broadcasted_iota(jnp.int32, (BLOCK, tok_rows), 0)
            column = lax.broadcasted_iota(jnp.int32, (BLOCK, tok_rows), 1)
            same = lax.rem(row, PAGE) == lax.rem(column, PAGE)
            self.onehot[pl.ds(pl.multiple_of(at, BLOCK), BLOCK), :] = jnp.where(
                same, spread, 0.0
            ).astype(jnp.bfloat16)
            return carry

        lax.fori_loop(0, REGIONS, hot, 0)

    def angles(self, at, rows_here):
        def turn(i, carry):
            row_at = pl.multiple_of(at + i * 64, 64)
            row = lax.broadcasted_iota(jnp.int32, (64, HEAD), 0) + (self.first + row_at)
            lane = lax.broadcasted_iota(jnp.int32, (64, HEAD), 1)
            angle = row.astype(jnp.float32) * self.freq[...]
            self.cosine[pl.ds(row_at, 64), :] = jnp.cos(angle)
            sined = jnp.sin(angle)
            self.sine[pl.ds(row_at, 64), :] = jnp.where(lane < HEAD // 2, -sined, sined)
            return carry

        lax.fori_loop(0, rows_here // 64, turn, 0)

    def project(self, weights, is_key, put):
        raw = jnp.dot(self.xbuf[...], weights, preferred_element_type=jnp.float32)
        if is_key:
            heads = []
            for head in range(weights.shape[1] // HEAD):
                one = raw[:, head * HEAD : (head + 1) * HEAD]
                heads.append(one * self.cosine[...] + pltpu.roll(one, HEAD // 2, 1) * self.sine[...])
            raw = jnp.concatenate(heads, axis=1)
        placed = jnp.dot(self.onehot[...], raw.astype(jnp.bfloat16), preferred_element_type=jnp.float32)
        put(placed.astype(jnp.bfloat16))


def copy_to(ref, send_sem, recv_sem, group_at, seq_at, dst=None):
    pltpu.make_async_remote_copy(
        src_ref=ref,
        dst_ref=ref if dst is None else dst,
        send_sem=send_sem,
        recv_sem=recv_sem,
        device_id={"group": group_at, "seq": seq_at},
        device_id_type=MESH,
    ).start()


def wait(ref, sem):
    pltpu.make_async_copy(ref, ref, sem).wait()


def line_kernel(
    n, tokens, gain, w_key, w_value, lengths, pages, freq, out,
    wide_gain, wbuf, xbuf, pbuf, rbuf, onehot, cosine, sine,
    load_sem, tok_sem, ys, yr, fr, fq, zi, zo, zr, xs, xo, xr, xq, cs, cr, hs, hr, rs, rr,
):
    chunks, depth = wbuf.shape[0], wbuf.shape[1]
    half, width = wbuf.shape[5], wbuf.shape[6]
    per_kind = chunks // 2
    group = lax.axis_index("group")
    me = lax.axis_index("seq")
    core, y, z = lax.rem(me, 2), lax.rem(me // 2, 2), me // 4
    other_core, other_y, other_group = 1 - core, 1 - y, 1 - group
    high = z // (depth // 2)
    is_end = (z == 0) | (z == depth - 1)

    def at(p):
        return p + high * (depth - 1 - 2 * p)

    def seq_of(z_at, y_at, core_at):
        return (z_at * 2 + y_at) * 2 + core_at

    to_y = seq_of(z, other_y, core)
    to_core = seq_of(z, y, other_core)

    def piece(j, zz, yy, part):
        return wbuf.at[j, zz, yy, core, part]

    def line(j, zz, yy):
        return wbuf.at[j, zz, yy, core]

    def pair(j, zz, part):
        return wbuf.at[j, zz, :, core, part]

    def layer(j, zz):
        return wbuf.at[j, zz, :, core]

    def load(j):
        w_ref = w_key if j < per_kind else w_value
        columns = pl.ds((j % per_kind) * width, width)
        return [
            pltpu.make_async_copy(
                w_ref.at[pl.ds(part * half, half), columns], piece(j, z, y, part), load_sem.at[j, part]
            )
            for part in range(2)
        ]

    for j in range(chunks):
        for copy in load(j):
            copy.start()
    token_copy = pltpu.make_async_copy(tokens, xbuf, tok_sem)
    token_copy.start()

    barrier = pltpu.get_barrier_semaphore()

    def greet(group_at, seq_at):
        pl.semaphore_signal(
            barrier, inc=1, device_id={"group": group_at, "seq": seq_at}, device_id_type=MESH
        )

    greet(other_group, me)
    for step in range(1, n):
        greet(group, lax.rem(me + step, n))
    pl.semaphore_wait(barrier, n)

    def over_y(ref, j, sem):
        copy_to(ref, ys.at[j], sem, group, to_y)

    def over_x(ref, j, sem):
        copy_to(ref, xs.at[j], sem, other_group, me)

    def inward(ref, j, zz, p):
        copy_to(ref, zi.at[j], zr.at[j, zz], group, seq_of(at(p), y, core))

    def outward(ref, j, zz):
        copy_to(ref, zo.at[j], zr.at[j, zz], group, seq_of(at(0), y, core))

    def to_partner(j, zz):
        copy_to(layer(j, zz), cs.at[j], cr.at[j], group, to_core)

    def loaded(j):
        for copy in load(j):
            copy.wait()

    def end_waits(j, what, k):
        form, both = CHUNKS[j]
        zz = at(k)
        if what == CROSS:
            return [(line(j, z, other_y) if both else piece(j, z, other_y, group), yr.at[j])]
        if what == ACROSS:
            return [(piece(j, z, other_y, other_group), xo.at[j])]
        if what == ALONG:
            return [(pair(j, zz, group) if form == PAIRED else piece(j, zz, y, group), zr.at[j, zz])]
        from_x = (piece(j, zz, y, other_group), xr.at[j, zz])
        from_y = (piece(j, zz, other_y, group), fr.at[j, zz])
        if what == FACE:
            return [(pair(j, zz, other_group), xr.at[j, zz])] if form == PAIRED else [from_x]
        if what == SIDE:
            return [from_y]
        if form == SPLIT:
            return [from_y, (piece(j, zz, other_y, other_group), fq.at[j, zz])]
        return [from_x, (piece(j, zz, other_y, other_group), xq.at[j, zz])]

    def end_sends(j, what, k):
        form, both = CHUNKS[j]
        zz = at(k)
        partner = functools.partial(to_partner, j, zz)
        if what == BEGIN:
            mine = line(j, z, y) if both else piece(j, z, y, group)
            return [lambda: over_y(mine, j, yr.at[j]), lambda: inward(line(j, z, y), j, z, 1)]
        if what == CROSS:
            if both:
                return [lambda: inward(line(j, z, other_y), j, z, 1), lambda: to_partner(j, z)]
            return [
                lambda: inward(piece(j, z, other_y, group), j, z, 1),
                lambda: over_x(piece(j, z, other_y, group), j, xo.at[j]),
            ]
        if what == ACROSS:
            return [lambda: inward(piece(j, z, other_y, other_group), j, z, 1), lambda: to_partner(j, z)]
        if what == ALONG:
            one = piece(j, zz, y, group)
            by_x = lambda: over_x(one, j, xr.at[j, zz])
            by_y = lambda: over_y(one, j, fr.at[j, zz])
            if form == PAIRED:
                return [lambda: over_x(pair(j, zz, group), j, xr.at[j, zz])]
            return [by_x, by_y] if form == SPLIT else [by_y, by_x]
        if what == FACE and form == SPLIT:
            return [lambda: over_y(piece(j, zz, y, other_group), j, fq.at[j, zz])]
        if what == SIDE:
            return [lambda: over_x(piece(j, zz, other_y, group), j, xq.at[j, zz])]
        return [partner]

    def inner_waits(j, what, p):
        zz = at(p)
        if what == CROSS:
            return [(piece(j, z, other_y, group), yr.at[j])]
        if what == ACROSS:
            return [(piece(j, z, other_y, other_group), xo.at[j])]
        if what == ALONG:
            return [(layer(j, zz) if p == 0 else pair(j, zz, group), zr.at[j, zz])]
        return [(pair(j, zz, other_group), xr.at[j, zz])]

    def inner_sends(j, what, p):
        form, _ = CHUNKS[j]
        zz = at(p)
        if what == BEGIN:
            mine = piece(j, z, y, group)
            return [
                lambda: over_y(mine, j, yr.at[j]),
                lambda: outward(mine, j, z),
                lambda: inward(mine, j, z, 2),
            ]
        if what == CROSS:
            crossed = piece(j, z, other_y, group)
            out_too = [lambda: outward(crossed, j, z)] if form == PAIRED else []
            return [lambda: inward(crossed, j, z, 2)] + out_too + [lambda: over_x(crossed, j, xo.at[j])]
        if what == ACROSS:
            return [lambda: to_partner(j, z)]
        if what == ALONG and p == 0:
            return [lambda: inward(pair(j, zz, group), j, zz, 2), lambda: to_partner(j, zz)]
        if what == ALONG:
            kept = pair(j, zz, group) if form == PAIRED else piece(j, zz, y, group)
            return [lambda: outward(kept, j, zz), lambda: over_x(pair(j, zz, group), j, xr.at[j, zz])]
        return [lambda: to_partner(j, zz)]

    first_chunk = [sum(GROUPS[:g]) for g in range(len(GROUPS))]

    def spot(g, region):
        j, wide = first_chunk[g], GROUPS[g] * width
        rows = pl.ds(region * BLOCK, BLOCK)
        return (
            pbuf.at[g, rows, pl.ds(0, wide)],
            out.at[j // per_kind, rows, pl.ds((j % per_kind) * width, wide)],
        )

    def page_to(g, region):
        src, dst = spot(g, region)
        there = lax.rem(me + region - REACH + n, n)
        z_there, y_there = there // 4, lax.rem(there // 2, 2)

        def direct():
            copy_to(src, hs.at[g, region], hr.at[g, region], group, there, dst)

        if g not in RELAYED:
            direct()
            return
        slot = 0 if abs(region - REACH) == 2 else 1
        around = ((z_there == 0) | (z_there == depth - 1)) & (z_there != z)
        z_by = 1 + (z_there // (depth - 1)) * (depth - 3)
        by = seq_of(z_by, y_there, lax.rem(there, 2))

        @pl.when(around)
        def _():
            held = rbuf.at[RELAYED.index(g), slot, :, pl.ds(0, GROUPS[g] * width)]
            copy_to(src, hs.at[g, region], rr.at[g, slot], group, by, held)

        @pl.when(jnp.logical_not(around))
        def _():
            direct()

    def pages_on_chip(g):
        src, dst = spot(g, REACH)
        pltpu.make_async_copy(src, dst, hr.at[g, REACH]).start()
        for region, on in ((3, core == 0), (1, core == 1)):
            @pl.when(on)
            def _():
                src, dst = spot(g, region)
                copy_to(src, hs.at[g, region], hr.at[g, region], group, to_core, dst)

    def pages_off_chip(g, way):
        page_to(g, 4 if way == UP else 0)

        @pl.when(core == (1 if way == UP else 0))
        def _():
            page_to(g, 3 if way == UP else 1)

    def pass_pages(g):
        def one(slot, region):
            held = rbuf.at[RELAYED.index(g), slot, :, pl.ds(0, GROUPS[g] * width)]
            wait(held, rr.at[g, slot])
            _, dst = spot(g, region)
            copy_to(held, rs.at[g, slot], hr.at[g, region], group, seq_of(at(0), y, core), dst)

        for side, regions in ((0, (4, 3)), (1, (0, 1))):
            @pl.when(y == side)
            def _():
                one(0, regions[0])

                @pl.when(core == side)
                def _():
                    one(1, regions[1])

    def run(steps, waits, sends, seen):
        for what, j, k, which in steps:
            if what in (UP, DOWN):
                pages_off_chip(j, what)
            elif what == RELAY:
                pass_pages(j)
            elif what == BEGIN:
                if j not in seen:
                    seen.add(j)
                    loaded(j)
                sends(j, what, k)[which]()
            elif which < 0:
                for ref, sem in waits(j, what, k):
                    wait(ref, sem)
            else:
                sends(j, what, k)[which]()

    work = Work(n, (gain, lengths, pages, freq, wide_gain, xbuf, onehot, cosine, sine), me)
    tok_rows = work.tok_rows

    def project(g):
        at_chunk, wide = first_chunk[g], GROUPS[g] * width
        blocks = []
        for j in range(at_chunk, at_chunk + GROUPS[g]):
            wait(wbuf.at[j, :, :, other_core], cr.at[j])
            blocks.append(wbuf[j].reshape(work.features, width))
        weights = blocks[0] if len(blocks) == 1 else jnp.concatenate(blocks, axis=1)

        def put(placed):
            pbuf[g, :, 0:wide] = placed

        work.project(weights, at_chunk < per_kind, put)
        pages_on_chip(g)

    sixteenth = tok_rows // 16
    jobs = [lambda: (work.spread_gain(), token_copy.wait())]
    jobs += [functools.partial(work.normalise, i * sixteenth, sixteenth) for i in range(16)]
    jobs += [work.mark_rows]
    jobs += [functools.partial(work.angles, i * (tok_rows // 2), tok_rows // 2) for i in range(2)]
    jobs, projects = iter(jobs), iter(range(len(GROUPS)))
    seen_end, seen_inner = set(), set()
    for stretch in range(len(COMPUTE) + 1):
        if stretch:
            if COMPUTE[stretch - 1]:
                project(next(projects))
            else:
                next(jobs)()
        if END[stretch]:

            @pl.when(is_end)
            def _():
                run(END[stretch], end_waits, end_sends, seen_end)

        if INNER[stretch]:

            @pl.when(jnp.logical_not(is_end))
            def _():
                run(INNER[stretch], inner_waits, inner_sends, seen_inner)

    def count(pieces, sem):
        wait(xbuf.at[pl.ds(0, half), pl.ds(0, pieces * width)], sem)

    for j in range(chunks):
        form, both = CHUNKS[j]
        wait(wbuf.at[j, :, :, core], cs.at[j])

        @pl.when(is_end)
        def _():
            far = depth - 1
            count((2 if both else 1) + far * {PAIRED: 0, SPLIT: 2, TURNED: 1}[form], ys.at[j])
            count(far * {PAIRED: 2, SPLIT: 1, TURNED: 2}[form] + (0 if both else 1), xs.at[j])
            count(4, zi.at[j])

        @pl.when(jnp.logical_not(is_end))
        def _():
            count(1, ys.at[j])
            count(2 * depth - 3, xs.at[j])
            count(4, zi.at[j])
            count((depth - 1) * (2 if form == PAIRED else 1), zo.at[j])

    for g in range(len(GROUPS)):
        for region in range(REGIONS):
            src, dst = spot(g, region)
            wait(dst, hr.at[g, region])
            if region != REACH:
                wait(src, hs.at[g, region])
        if g in RELAYED:
            held = rbuf.at[RELAYED.index(g), 0, :, pl.ds(0, GROUPS[g] * width)]

            @pl.when(jnp.logical_not(is_end))
            def _():
                wait(held, rs.at[g, 0])

                @pl.when(core == y)
                def _():
                    wait(held, rs.at[g, 1])


def loop_kernel(
    n, tokens, gain, w_key, w_value, lengths, pages, freq, out,
    wide_gain, wbuf, xbuf, pbuf, onehot, cosine, sine,
    load_sem, tok_sem, ys, yr, zs, zr, xs, xr, cs, cr, hs, hr,
):
    chunks, depth = wbuf.shape[0], wbuf.shape[1]
    half, width = wbuf.shape[5], wbuf.shape[6]
    per_kind = chunks // 2
    group = lax.axis_index("group")
    me = lax.axis_index("seq")
    core, y, z = lax.rem(me, 2), lax.rem(me // 2, 2), me // 4
    other_core, other_y, other_group = 1 - core, 1 - y, 1 - group

    def seq_of(z_at, y_at, core_at):
        return (z_at * 2 + y_at) * 2 + core_at

    def piece(j, z_at, y_at, part):
        return wbuf.at[j, z_at, y_at, core, part]

    loads = []
    for j in range(chunks):
        w_ref = w_key if j < per_kind else w_value
        columns = pl.ds((j % per_kind) * width, width)
        for part in range(2):
            copy = pltpu.make_async_copy(
                w_ref.at[pl.ds(part * half, half), columns], piece(j, z, y, part), load_sem.at[j, part]
            )
            copy.start()
            loads.append(copy)
    token_copy = pltpu.make_async_copy(tokens, xbuf, tok_sem)
    token_copy.start()

    to_y = seq_of(z, other_y, core)
    to_core = seq_of(z, y, other_core)
    has_up, has_down = z + 1 < depth, z > 0
    up = seq_of(lax.rem(z + 1, depth), y, core)
    down = seq_of(lax.rem(z + depth - 1, depth), y, core)

    barrier = pltpu.get_barrier_semaphore()

    def greet(group_at, seq_at):
        pl.semaphore_signal(
            barrier, inc=1, device_id={"group": group_at, "seq": seq_at}, device_id_type=MESH
        )

    for seq_at in (up, down, to_y, to_core):
        greet(group, seq_at)
    greet(other_group, me)
    for region in range(REGIONS):
        if region != REACH:
            greet(group, lax.rem(me + region - REACH + n, n))
    pl.semaphore_wait(barrier, 5 + REGIONS - 1)

    def to_partner(j, ref):
        copy_to(ref, cs.at[j], cr.at[j], group, to_core)

    def go(j, z_at, y_at, k, way):
        @pl.when(has_up if way == 0 else has_down)
        def _():
            copy_to(piece(j, z_at, y_at, group), zs.at[j, way, k], zr.at[j, y_at, z_at], group,
                    up if way == 0 else down)

    def begin(j):
        for part in (0, 1):
            loads[2 * j + part].wait()
        for part in (0, 1):
            copy_to(piece(j, z, y, part), ys.at[j], yr.at[j, part], group, to_y)
            to_partner(j, piece(j, z, y, part))
        go(j, z, y, 0, 0)
        go(j, z, y, 0, 1)

    def cross(j):
        for part in (0, 1):
            wait(piece(j, z, other_y, part), yr.at[j, part])
            to_partner(j, piece(j, z, other_y, part))
        go(j, z, other_y, 0, 0)
        go(j, z, other_y, 0, 1)

    def both(k, visit):
        @pl.when(z - k >= 0)
        def _():
            visit(z - k, 0)

        @pl.when(z + k < depth)
        def _():
            visit(z + k, 1)

    def along(j, k):
        def visit(zz, way):
            for y_at in (y, other_y):
                ref = piece(j, zz, y_at, group)
                wait(ref, zr.at[j, y_at, zz])
                go(j, zz, y_at, k, way)
                copy_to(ref, xs.at[j], xr.at[j, y_at, zz], other_group, me)
                to_partner(j, ref)

        both(k, visit)

    def finish(j, k):
        def visit(zz, way):
            for y_at in (y, other_y):
                ref = piece(j, zz, y_at, other_group)
                wait(ref, xr.at[j, y_at, zz])
                to_partner(j, ref)

        both(k, visit)

    work = Work(n, (gain, lengths, pages, freq, wide_gain, xbuf, onehot, cosine, sine), me)

    def project(j):
        wait(wbuf.at[j, :, :, other_core], cr.at[j])
        for at in range(0, width, TILE):
            def put(placed):
                pbuf[j, :, at : at + TILE] = placed

            weights = wbuf[j, :, :, :, :, :, at : at + TILE].reshape(work.features, TILE)
            work.project(weights, j < per_kind, put)

    def spot(j, region):
        rows = pl.ds(region * BLOCK, BLOCK)
        return (
            pbuf.at[j, rows, :],
            out.at[j // per_kind, rows, pl.ds((j % per_kind) * width, width)],
        )

    def hand_over(j):
        for region in range(REGIONS):
            src, dst = spot(j, region)
            if region == REACH:
                pltpu.make_async_copy(src, dst, hr.at[j, region]).start()
            else:
                copy_to(src, hs.at[j, region], hr.at[j, region], group,
                        lax.rem(me + region - REACH + n, n), dst)

    for j in range(chunks):
        begin(j)
    work.spread_gain()
    token_copy.wait()
    work.normalise(0, work.tok_rows)
    work.mark_rows()
    work.angles(0, work.tok_rows)
    for j in range(chunks):
        cross(j)
        lax.fori_loop(1, depth, lambda k, carry: (along(j, k), carry)[1], 0)
        lax.fori_loop(1, depth, lambda k, carry: (finish(j, k), carry)[1], 0)
        project(j)
        hand_over(j)

    for j in range(chunks):
        wait(wbuf.at[j, z, y, core], ys.at[j])
        wait(wbuf.at[j, 1:, :, core, group], xs.at[j])
        wait(wbuf.at[j, :, :, core], cs.at[j])
        sent = wbuf.at[j, 0, :, core, group]

        def drain(k, carry):
            @pl.when(has_up & (z - k >= 0))
            def _():
                wait(sent, zs.at[j, 0, k])

            @pl.when(has_down & (z + k < depth))
            def _():
                wait(sent, zs.at[j, 1, k])

            return carry

        lax.fori_loop(0, depth, drain, 0)
        for region in range(REGIONS):
            src, dst = spot(j, region)
            wait(dst, hr.at[j, region])
            if region != REACH:
                wait(src, hs.at[j, region])


def on_device(n, tokens, norm_gain, w_key, w_value, lengths, page_table):
    tok_rows, features = tokens.shape
    columns = w_key.shape[1]
    freq = ROPE_THETA ** (-(np.arange(HEAD // 2) * 2.0 / HEAD))
    freq = np.concatenate([freq, freq]).astype(np.float32)[None, :]
    depth = n // 4
    half = w_key.shape[0] // 2
    dma = pltpu.SemaphoreType.DMA
    vmem = pl.BlockSpec(memory_space=pltpu.VMEM)
    smem = pl.BlockSpec(memory_space=pltpu.SMEM)
    hbm = pl.BlockSpec(memory_space=pl.ANY)
    in_line = depth == LAYERS
    chunks = len(CHUNKS) if in_line else LOOP_CHUNKS
    groups = len(GROUPS) if in_line else chunks
    width = 2 * columns // chunks
    wide = width * max(GROUPS) if in_line else width
    scratch = [
        pltpu.VMEM((1, features), jnp.float32),
        pltpu.VMEM((chunks, depth, 2, 2, 2, half, width), jnp.bfloat16),
        pltpu.VMEM((tok_rows, features), jnp.bfloat16),
        pltpu.VMEM((groups, ROWS, wide), jnp.bfloat16),
    ]
    if in_line:
        scratch.append(pltpu.VMEM((max(len(RELAYED), 1), 2, BLOCK, wide), jnp.bfloat16))
    scratch += [
        pltpu.VMEM((ROWS, tok_rows), jnp.bfloat16),
        pltpu.VMEM((tok_rows, HEAD), jnp.float32),
        pltpu.VMEM((tok_rows, HEAD), jnp.float32),
        dma((chunks, 2)),
        dma,
    ]
    each, by_layer, by_region = dma((chunks,)), dma((chunks, depth)), dma((groups, REGIONS))
    if in_line:
        slots = dma((groups, 2))
        scratch += [each, each, by_layer, by_layer, each, each, by_layer, each, each, by_layer, by_layer,
                    each, each, by_region, by_region, slots, slots]
    else:
        by_line = dma((chunks, 2, depth))
        scratch += [each, dma((chunks, 2)), by_line, by_line, each, by_line, each, each,
                    by_region, by_region]
    cache = pl.pallas_call(
        functools.partial(line_kernel if in_line else loop_kernel, n),
        out_shape=jax.ShapeDtypeStruct((2, ROWS, columns), jnp.bfloat16),
        in_specs=[hbm, vmem, hbm, hbm, smem, vmem, vmem],
        out_specs=hbm,
        scratch_shapes=scratch,
        compiler_params=pltpu.CompilerParams(
            collective_id=0, has_side_effects=True, vmem_limit_bytes=60 * 2**20
        ),
    )(tokens, norm_gain.reshape(-1, HEAD), w_key, w_value, lengths, page_table[None, :], freq)
    return cache.reshape(2, SLOTS, PAGE, columns)


def solution(mesh):
    placed = (
        P(("group", "seq"), None),
        P(),
        P("seq", None),
        P("seq", None),
        P("group"),
        P(("group", "seq")),
    )
    return jax.shard_map(
        functools.partial(on_device, mesh.shape["seq"]),
        mesh=mesh,
        in_specs=placed,
        out_specs=P(None, ("group", "seq"), None, None),
        check_vma=False,
    )
```

time: 101 us -> 101 us (level)
  Pallas kernels: 96.1 us -> 97.5 us
  local copies, waits for them, and re-layouts: 4.98 us -> 3.67 us
    pallas_call x1, Pallas kernels: 96.1 us -> 97.5 us  [on_device(): pl.pallas_call(functools.partial(line_kernel if in_line else loop_kernel,...]
    broadcast_in_dim x1 -> x0, local copies, waits for them, and re-layouts: 1.31 us -> none  [on_device(): norm_gain[None, :]]
where the time goes in v1:
time: 101 us
  Pallas kernels  97.5 us (97%)
  local copies, waits for them, and re-layouts  3.67 us (4%)
    pallas_call x1, Pallas kernels, on_device(): pl.pallas_call(functools.partial(line_kernel if in_line else loop_kernel,...  97.5 us
    unnamed x1, local copies, waits for them, and re-layouts  3.67 us

profile of v1, /device:TPU:1, one launch (start us, length us, event | category | flops | bytes accessed | tf_op | source)
XLA Modules:
  0.0 101.2 jit_solution(14588021749225858310)
XLA Ops:
  0.0 97.5 %shard_map.73 = bf16[2,640,1024]{2,1,0:T(8,128)(2,1)} custom-call(bf16[512,4096]{1,0:T(8,128)(2,1)} %tokens.1, bf16[32,128]{1,0:T(8,128)(2,1)} %bitcast.4, bf16[256,1024]{1,0:T(8,128)(2,1)} %w_key.1, bf16[256,1024]{1,0:T(8,128)(2,1)} %w_value.1, s32[2]{0:T(128)} %lengths.1, s32[1,32]{1,0:T(1,128)} %bitcast.5, f32[1,128]{1,0:T(1,128)} %constant.2.clone.freq), custom_call_target="tpu_custom_call" | custom-call | tf_op jit(solution)/shard_map/pallas_call | solution.py:783
  97.5 3.7 %copy.9 = bf16[2,40,16,1024]{3,2,1,0:T(8,128)(2,1)} copy(bf16[2,40,16,1024]{3,2,1,0:T(8,128)(2,1)} %bitcast.3) | data formatting | bytes 5242880

commit v2 on v1

--- a/solution.py
+++ b/solution.py
@@ -33,123 +33,255 @@
 
 BEGIN, CROSS, ACROSS, ALONG, FACE, SIDE, SETTLE, UP, DOWN, RELAY = range(10)
 COMPUTE = (0,0,0,0,0,0,0,0,0,0,0,0,0,0,0,0,0,0,0,0,1,1,1,1,1,1,1,1)
-END = (
-    ((BEGIN, 0, 0, 0), (BEGIN, 0, 0, 1), (BEGIN, 1, 0, 0), (BEGIN, 1, 0, 1), (BEGIN, 2, 0, 0),),
-    (),
-    (),
-    (),
-    (),
-    (),
+END_FIRST = (
+    ((BEGIN, 0, 0, 0), (BEGIN, 0, 0, 1),),
+    (),
+    (),
+    ((BEGIN, 1, 0, 0),),
+    (),
+    (),
+    ((BEGIN, 1, 0, 1),),
+    (),
+    (),
+    (),
+    (),
+    (),
+    (),
+    (),
+    ((BEGIN, 2, 0, 0),),
+    (),
+    (),
+    ((ALONG, 0, 1, -1), (ALONG, 0, 1, 0), (ALONG, 0, 1, 1),),
+    (),
+    ((CROSS, 0, 0, -1), (CROSS, 0, 0, 0), (CROSS, 0, 0, 1),),
+    ((CROSS, 1, 0, -1), (CROSS, 1, 0, 0), (CROSS, 1, 0, 1), (FACE, 0, 1, -1), (FACE, 0, 1, 0), (BEGIN, 3, 0, 0),
+     (ALONG, 3, 1, -1), (ALONG, 3, 1, 0), (ACROSS, 1, 0, -1), (ACROSS, 1, 0, 0), (ACROSS, 1, 0, 1),
+     (ALONG, 1, 1, -1), (ALONG, 1, 1, 0), (BEGIN, 2, 0, 1), (CROSS, 2, 0, -1), (CROSS, 2, 0, 1),
+     (SETTLE, 0, 1, -1), (SETTLE, 0, 1, 0), (ALONG, 2, 1, -1), (ALONG, 2, 1, 0), (ALONG, 3, 1, 1),
+     (ALONG, 0, 2, -1), (ALONG, 0, 2, 1), (CROSS, 2, 0, 0), (FACE, 1, 1, -1), (FACE, 1, 1, 0), (FACE, 3, 1, -1),
+     (FACE, 3, 1, 0), (ALONG, 0, 2, 0), (ALONG, 1, 2, -1), (ALONG, 1, 2, 0), (CROSS, 3, 0, -1),
+     (CROSS, 3, 0, 1), (BEGIN, 4, 0, 0), (BEGIN, 3, 0, 1), (ALONG, 2, 2, -1), (FACE, 2, 1, -1),
+     (FACE, 2, 1, 0), (SETTLE, 3, 1, -1), (SETTLE, 3, 1, 0), (ALONG, 2, 2, 0), (ALONG, 3, 2, -1),
+     (FACE, 0, 2, -1), (FACE, 0, 2, 0), (CROSS, 3, 0, 0), (ALONG, 0, 3, -1), (ALONG, 3, 2, 1), (ALONG, 0, 3, 1),
+     (FACE, 1, 2, -1), (FACE, 1, 2, 0), (ALONG, 0, 3, 0), (CROSS, 4, 0, -1), (CROSS, 4, 0, 1), (BEGIN, 4, 0, 1),
+     (BEGIN, 5, 0, 0), (ALONG, 3, 2, 0), (CROSS, 4, 0, 0), (FACE, 2, 2, -1), (FACE, 2, 2, 0), (SETTLE, 0, 2, -1),
+     (SETTLE, 0, 2, 0), (FACE, 0, 3, -1), (FACE, 0, 3, 0), (BEGIN, 5, 0, 1), (ALONG, 1, 3, -1),
+     (ALONG, 1, 3, 0), (FACE, 3, 2, -1), (FACE, 3, 2, 0), (ALONG, 4, 1, -1), (ALONG, 4, 1, 0), (BEGIN, 6, 0, 0),
+     (CROSS, 5, 0, -1), (CROSS, 5, 0, 1), (ALONG, 4, 2, -1), (ALONG, 4, 2, 0), (CROSS, 5, 0, 0),
+     (BEGIN, 7, 0, 0), (SETTLE, 0, 3, -1), (SETTLE, 0, 3, 0), (FACE, 1, 3, -1), (FACE, 1, 3, 0),
+     (BEGIN, 6, 0, 1), (ALONG, 2, 3, -1), (ALONG, 2, 3, 0), (ALONG, 5, 2, -1),),
+    (),
+    ((SETTLE, 3, 2, -1), (SETTLE, 3, 2, 0), (ALONG, 5, 1, -1), (ALONG, 5, 1, 1), (FACE, 4, 1, -1),
+     (FACE, 4, 1, 0), (ALONG, 5, 2, 1), (ALONG, 3, 3, -1), (ALONG, 3, 3, 1), (ALONG, 3, 3, 0), (ALONG, 5, 1, 0),
+     (CROSS, 6, 0, -1), (CROSS, 6, 0, 1), (CROSS, 6, 0, 0), (FACE, 4, 2, -1), (FACE, 4, 2, 0), (CROSS, 7, 0, -1),
+     (CROSS, 7, 0, 1), (ALONG, 5, 2, 0), (BEGIN, 7, 0, 1), (FACE, 2, 3, -1), (FACE, 2, 3, 0), (ALONG, 6, 1, -1),
+     (ALONG, 6, 1, 0), (DOWN, 0, 0, 0), (FACE, 3, 3, -1), (FACE, 3, 3, 0), (UP, 0, 0, 0),),
+    ((ALONG, 4, 3, -1), (UP, 0, 0, 1), (CROSS, 7, 0, 0), (ALONG, 4, 3, 0), (FACE, 5, 1, -1), (FACE, 5, 1, 0),
+     (FACE, 5, 2, -1), (FACE, 5, 2, 0), (SETTLE, 5, 1, -1), (SETTLE, 5, 1, 0), (DOWN, 0, 0, 1),
+     (SETTLE, 3, 3, -1), (SETTLE, 3, 3, 0), (ALONG, 6, 2, -1), (UP, 1, 0, 0), (FACE, 6, 1, -1),
+     (FACE, 6, 1, 0), (ALONG, 5, 3, -1), (ALONG, 5, 3, 0), (ALONG, 5, 3, 1), (ALONG, 6, 2, 0), (DOWN, 2, 0, 0),
+     (UP, 2, 0, 0), (FACE, 5, 3, -1), (FACE, 5, 3, 0), (FACE, 4, 3, -1), (FACE, 4, 3, 0), (DOWN, 1, 0, 1),
+     (SETTLE, 5, 2, -1), (SETTLE, 5, 2, 0), (ALONG, 7, 1, -1), (ALONG, 7, 1, 0), (UP, 1, 0, 1),
+     (DOWN, 2, 0, 1), (UP, 2, 0, 1),),
+    ((UP, 3, 0, 0), (DOWN, 1, 0, 0),),
+    ((DOWN, 3, 0, 1), (UP, 3, 0, 1), (UP, 4, 0, 0), (FACE, 6, 2, -1), (FACE, 6, 2, 0), (ALONG, 6, 3, -1),
+     (ALONG, 6, 3, 0), (DOWN, 3, 0, 0), (ALONG, 7, 2, -1), (ALONG, 7, 2, 0), (DOWN, 4, 0, 0), (SETTLE, 5, 3, -1),
+     (SETTLE, 5, 3, 0), (DOWN, 4, 0, 1), (UP, 4, 0, 1), (FACE, 7, 1, -1), (FACE, 7, 1, 0),),
+    ((UP, 5, 0, 0), (DOWN, 5, 0, 0), (ALONG, 7, 3, -1), (ALONG, 7, 3, 0), (UP, 5, 0, 1), (DOWN, 5, 0, 1),
+     (FACE, 6, 3, -1), (FACE, 6, 3, 0), (FACE, 7, 2, -1), (FACE, 7, 2, 0),),
+    ((DOWN, 6, 0, 0), (UP, 6, 0, 0), (UP, 6, 0, 1), (DOWN, 6, 0, 1), (FACE, 7, 3, -1), (FACE, 7, 3, 0),
+     ),
+    ((DOWN, 7, 0, 0), (DOWN, 7, 0, 1), (UP, 7, 0, 0), (UP, 7, 0, 1),),
+)
+END_SECOND = (
+    ((BEGIN, 0, 0, 0), (BEGIN, 0, 0, 1),),
+    (),
+    (),
+    (),
+    ((BEGIN, 1, 0, 0),),
+    ((BEGIN, 1, 0, 1),),
+    (),
+    (),
+    (),
+    (),
+    (),
+    (),
+    (),
+    (),
+    (),
+    ((BEGIN, 2, 0, 0),),
+    (),
+    (),
+    ((ALONG, 0, 1, -1), (ALONG, 0, 1, 0), (ALONG, 0, 1, 1),),
+    (),
+    ((CROSS, 0, 0, -1), (CROSS, 0, 0, 0), (CROSS, 0, 0, 1), (CROSS, 1, 0, -1), (CROSS, 1, 0, 0),
+     (CROSS, 1, 0, 1), (ALONG, 3, 1, -1), (ALONG, 3, 1, 0), (FACE, 0, 1, -1), (FACE, 0, 1, 0), (BEGIN, 3, 0, 0),
+     (ACROSS, 1, 0, -1), (ACROSS, 1, 0, 0), (ACROSS, 1, 0, 1), (ALONG, 1, 1, -1), (ALONG, 1, 1, 0),
+     (FACE, 3, 1, -1), (FACE, 3, 1, 0), (BEGIN, 2, 0, 1), (CROSS, 2, 0, -1), (CROSS, 2, 0, 1), (ALONG, 2, 1, -1),
+     (ALONG, 2, 1, 0), (ALONG, 3, 1, 1), (SETTLE, 0, 1, -1), (SETTLE, 0, 1, 0), (CROSS, 2, 0, 0),
+     (FACE, 1, 1, -1), (FACE, 1, 1, 0), (ALONG, 0, 2, -1), (ALONG, 0, 2, 1), (ALONG, 0, 2, 0), (BEGIN, 4, 0, 0),
+     (CROSS, 3, 0, -1), (CROSS, 3, 0, 1), (CROSS, 3, 0, 0), (BEGIN, 3, 0, 1), (ALONG, 1, 2, -1),
+     (ALONG, 1, 2, 0), (FACE, 2, 1, -1), (FACE, 2, 1, 0), (ALONG, 2, 2, -1), (ALONG, 2, 2, 0), (SETTLE, 3, 1, -1),
+     (SETTLE, 3, 1, 0), (FACE, 0, 2, -1), (FACE, 0, 2, 0), (ALONG, 3, 2, -1), (ALONG, 0, 3, -1),
+     (ALONG, 0, 3, 0), (ALONG, 0, 3, 1), (FACE, 1, 2, -1), (FACE, 1, 2, 0), (ALONG, 3, 2, 1), (BEGIN, 4, 0, 1),
+     (ALONG, 3, 2, 0), (ALONG, 4, 1, -1), (ALONG, 4, 1, 0), (BEGIN, 5, 0, 0), (CROSS, 4, 0, -1),
+     (CROSS, 4, 0, 0), (CROSS, 4, 0, 1), (SETTLE, 0, 2, -1), (SETTLE, 0, 2, 0), (FACE, 2, 2, -1),
+     (FACE, 2, 2, 0), (ALONG, 1, 3, -1), (ALONG, 1, 3, 0), (BEGIN, 5, 0, 1), (FACE, 0, 3, -1), (FACE, 0, 3, 0),
+     (FACE, 3, 2, -1), (FACE, 3, 2, 0), (BEGIN, 6, 0, 0), (CROSS, 5, 0, -1), (CROSS, 5, 0, 0), (CROSS, 5, 0, 1),
+     (ALONG, 4, 2, -1), (ALONG, 4, 2, 0), (SETTLE, 0, 3, -1), (SETTLE, 0, 3, 0), (FACE, 1, 3, -1),
+     (FACE, 1, 3, 0), (FACE, 4, 1, -1), (FACE, 4, 1, 0), (SETTLE, 3, 2, -1), (SETTLE, 3, 2, 0),
+     (BEGIN, 7, 0, 0), (ALONG, 2, 3, -1), (ALONG, 2, 3, 0), (ALONG, 5, 2, -1), (ALONG, 5, 2, 1),
+     (BEGIN, 6, 0, 1),),
+    (),
+    ((ALONG, 5, 1, -1), (ALONG, 5, 1, 1), (ALONG, 5, 2, 0), (ALONG, 3, 3, -1), (ALONG, 3, 3, 0),
+     (ALONG, 3, 3, 1), (ALONG, 5, 1, 0), (CROSS, 6, 0, -1), (CROSS, 6, 0, 0), (CROSS, 6, 0, 1),
+     (FACE, 4, 2, -1), (FACE, 4, 2, 0), (BEGIN, 7, 0, 1), (FACE, 2, 3, -1), (FACE, 2, 3, 0), (CROSS, 7, 0, -1),
+     (CROSS, 7, 0, 1), (ALONG, 6, 1, -1), (ALONG, 6, 1, 0), (DOWN, 0, 0, 0), (UP, 0, 0, 0), (UP, 1, 0, 1),
+     (CROSS, 7, 0, 0), (FACE, 3, 3, -1), (FACE, 3, 3, 0), (ALONG, 4, 3, -1), (ALONG, 4, 3, 0), (FACE, 5, 1, -1),
+     (FACE, 5, 1, 0), (FACE, 5, 2, -1), (FACE, 5, 2, 0), (SETTLE, 3, 3, -1), (SETTLE, 3, 3, 0),
+     (DOWN, 0, 0, 1), (UP, 0, 0, 1),),
+    ((DOWN, 1, 0, 0), (UP, 1, 0, 0), (ALONG, 5, 3, -1), (ALONG, 5, 3, 0), (ALONG, 5, 3, 1), (FACE, 6, 1, -1),
+     (FACE, 6, 1, 0), (ALONG, 6, 2, -1), (ALONG, 6, 2, 0), (DOWN, 1, 0, 1), (SETTLE, 5, 1, -1),
+     (SETTLE, 5, 1, 0), (DOWN, 2, 0, 0), (UP, 2, 0, 0),),
+    ((FACE, 4, 3, -1), (FACE, 4, 3, 0), (SETTLE, 5, 2, -1), (SETTLE, 5, 2, 0), (DOWN, 2, 0, 1),
+     (FACE, 5, 3, -1), (FACE, 5, 3, 0), (ALONG, 7, 1, -1), (ALONG, 7, 1, 0), (UP, 3, 0, 0), (UP, 2, 0, 1),
+     ),
+    ((DOWN, 3, 0, 1), (UP, 3, 0, 1), (FACE, 6, 2, -1), (FACE, 6, 2, 0), (ALONG, 6, 3, -1), (ALONG, 6, 3, 0),
+     (UP, 4, 0, 0), (DOWN, 3, 0, 0), (DOWN, 4, 0, 0), (SETTLE, 5, 3, -1), (SETTLE, 5, 3, 0), (UP, 4, 0, 1),
+     (DOWN, 4, 0, 1), (FACE, 7, 1, -1), (FACE, 7, 1, 0),),
+    ((DOWN, 5, 0, 0), (UP, 5, 0, 0), (UP, 5, 0, 1), (DOWN, 5, 0, 1), (ALONG, 7, 2, -1), (ALONG, 7, 2, 0),
+     (FACE, 6, 3, -1), (FACE, 6, 3, 0),),
+    ((UP, 6, 0, 0), (DOWN, 6, 0, 0), (ALONG, 7, 3, -1), (ALONG, 7, 3, 0), (UP, 6, 0, 1), (DOWN, 6, 0, 1),
+     (FACE, 7, 2, -1), (FACE, 7, 2, 0), (FACE, 7, 3, -1), (FACE, 7, 3, 0),),
+    ((DOWN, 7, 0, 0), (UP, 7, 0, 0), (DOWN, 7, 0, 1), (UP, 7, 0, 1),),
+)
+INNER_FIRST = (
+    ((BEGIN, 0, 0, 0), (BEGIN, 0, 0, 1), (BEGIN, 0, 0, 2), (BEGIN, 1, 0, 0),),
+    (),
+    ((BEGIN, 1, 0, 2), (BEGIN, 1, 0, 1),),
+    ((BEGIN, 2, 0, 0),),
+    (),
+    (),
+    ((BEGIN, 2, 0, 2),),
     ((BEGIN, 2, 0, 1),),
-    (),
-    ((BEGIN, 3, 0, 0), (ALONG, 0, 1, -1), (ALONG, 0, 1, 0), (ALONG, 0, 1, 1),),
+    ((BEGIN, 3, 0, 1),),
+    (),
+    ((BEGIN, 3, 0, 0),),
+    (),
+    (),
     ((CROSS, 0, 0, -1), (CROSS, 0, 0, 0), (CROSS, 0, 0, 1),),
     (),
-    (),
-    ((CROSS, 1, 0, -1), (CROSS, 1, 0, 0), (CROSS, 1, 0, 1),),
-    (),
-    ((FACE, 0, 1, -1), (FACE, 0, 1, 0),),
-    ((BEGIN, 3, 0, 1), (ALONG, 3, 1, -1), (ALONG, 3, 1, 0),),
     ((BEGIN, 4, 0, 0),),
-    ((ALONG, 3, 1, 1), (CROSS, 2, 0, -1), (CROSS, 2, 0, 1),),
-    ((CROSS, 2, 0, 0), (ALONG, 1, 1, -1), (ALONG, 1, 1, 0),),
-    ((ACROSS, 1, 0, -1), (ACROSS, 1, 0, 0), (ACROSS, 1, 0, 1),),
-    ((BEGIN, 4, 0, 1), (ALONG, 2, 1, -1), (ALONG, 2, 1, 0), (FACE, 3, 1, -1), (FACE, 3, 1, 0), (SETTLE, 0, 1, -1),
-     (SETTLE, 0, 1, 0), (BEGIN, 5, 0, 0), (ALONG, 0, 2, -1), (ALONG, 0, 2, 0), (ALONG, 0, 2, 1),
-     (BEGIN, 5, 0, 1), (CROSS, 3, 0, -1), (CROSS, 3, 0, 1), (FACE, 1, 1, -1), (FACE, 1, 1, 0), (ALONG, 1, 2, -1),
-     (ALONG, 1, 2, 0), (CROSS, 3, 0, 0), (BEGIN, 6, 0, 0), (FACE, 0, 2, -1), (FACE, 0, 2, 0), (BEGIN, 7, 0, 0),
-     (BEGIN, 6, 0, 1), (ALONG, 2, 2, -1), (ALONG, 2, 2, 0), (SETTLE, 3, 1, -1), (SETTLE, 3, 1, 0),
-     (FACE, 2, 1, -1), (FACE, 2, 1, 0), (ALONG, 3, 2, -1), (ALONG, 3, 2, 0), (ALONG, 3, 2, 1), (SETTLE, 0, 2, -1),
-     (SETTLE, 0, 2, 0), (BEGIN, 7, 0, 1), (ALONG, 0, 3, -1), (ALONG, 0, 3, 0), (ALONG, 0, 3, 1),
-     (FACE, 1, 2, -1), (FACE, 1, 2, 0), (CROSS, 4, 0, -1), (CROSS, 4, 0, 0), (CROSS, 4, 0, 1), (ALONG, 4, 1, -1),
-     (ALONG, 4, 1, 0), (FACE, 2, 2, -1), (FACE, 2, 2, 0), (FACE, 0, 3, -1), (FACE, 0, 3, 0), (ALONG, 4, 2, -1),
-     (ALONG, 4, 2, 0), (FACE, 3, 2, -1), (FACE, 3, 2, 0), (CROSS, 5, 0, -1), (CROSS, 5, 0, 0), (CROSS, 5, 0, 1),
-     (ALONG, 1, 3, -1), (ALONG, 1, 3, 0), (SETTLE, 0, 3, -1), (SETTLE, 0, 3, 0), (FACE, 4, 1, -1),
-     (FACE, 4, 1, 0), (SETTLE, 3, 2, -1), (SETTLE, 3, 2, 0), (ALONG, 2, 3, -1), (ALONG, 2, 3, 0),
+    (),
+    ((CROSS, 1, 0, -1), (CROSS, 1, 0, 0), (CROSS, 1, 0, 1), (CROSS, 1, 0, 2),),
+    (),
+    ((BEGIN, 5, 0, 0),),
+    ((CROSS, 2, 0, -1), (CROSS, 2, 0, 0), (CROSS, 2, 0, 2), (CROSS, 2, 0, 1), (ACROSS, 0, 0, -1),
+     (ACROSS, 0, 0, 0), (CROSS, 3, 0, -1), (CROSS, 3, 0, 0), (CROSS, 3, 0, 1), (BEGIN, 6, 0, 0),
+     (BEGIN, 3, 0, 2), (ALONG, 0, 2, -1), (ALONG, 0, 2, 0), (ALONG, 0, 2, 1), (BEGIN, 7, 0, 0),
+     (ACROSS, 1, 0, -1), (ACROSS, 1, 0, 0), (CROSS, 4, 0, -1), (ALONG, 1, 2, -1), (ALONG, 1, 2, 0),
+     (ALONG, 1, 2, 1), (ACROSS, 2, 0, -1), (ACROSS, 2, 0, 0), (ALONG, 0, 0, -1), (ALONG, 0, 0, 0),
+     (ALONG, 0, 0, 1), (ALONG, 2, 2, -1), (ALONG, 2, 2, 0), (CROSS, 5, 0, -1), (ALONG, 2, 2, 1),
+     (CROSS, 6, 0, -1), (ACROSS, 3, 0, -1), (ACROSS, 3, 0, 0), (ALONG, 3, 2, -1), (ALONG, 1, 0, -1),
+     (ALONG, 1, 0, 0), (ALONG, 1, 0, 1), (CROSS, 4, 0, 0), (FACE, 0, 2, -1), (FACE, 0, 2, 0), (CROSS, 7, 0, -1),
+     (ALONG, 3, 2, 0), (ALONG, 0, 3, -1), (ALONG, 0, 3, 0), (BEGIN, 4, 0, 2), (ALONG, 0, 3, 1),
+     (BEGIN, 4, 0, 1), (FACE, 1, 2, -1), (FACE, 1, 2, 0), (ALONG, 2, 0, -1), (ALONG, 2, 0, 0), (ALONG, 2, 0, 1),
+     (CROSS, 4, 0, 1), (FACE, 2, 2, -1), (FACE, 2, 2, 0), (ALONG, 1, 3, -1), (ALONG, 1, 3, 0), (ALONG, 1, 3, 1),
+     (ALONG, 3, 2, 1), (CROSS, 5, 0, 0), (CROSS, 4, 0, 2), (BEGIN, 5, 0, 2), (FACE, 0, 3, -1), (FACE, 0, 3, 0),
+     (ALONG, 4, 2, -1), (ALONG, 4, 2, 0), (FACE, 1, 3, -1), (FACE, 1, 3, 0), (BEGIN, 6, 0, 2), (ALONG, 3, 0, -1),
+     (ALONG, 3, 0, 0), (ALONG, 3, 0, 1), (ALONG, 2, 3, -1), (ALONG, 2, 3, 0), (ALONG, 2, 3, 1),
+     (CROSS, 6, 0, 0), (ALONG, 4, 2, 1), (BEGIN, 5, 0, 1),),
+    ((FACE, 3, 2, -1), (FACE, 3, 2, 0), (ALONG, 5, 2, -1), (ALONG, 5, 2, 0),),
+    ((UP, 1, 0, 1), (BEGIN, 6, 0, 1), (ALONG, 4, 0, -1), (ALONG, 4, 0, 0), (ALONG, 4, 0, 1), (ACROSS, 4, 0, -1),
+     (ACROSS, 4, 0, 0), (ALONG, 3, 3, -1), (ALONG, 3, 3, 0), (ALONG, 3, 3, 1), (UP, 1, 0, 0), (FACE, 2, 3, -1),
+     (FACE, 2, 3, 0), (ALONG, 6, 2, -1), (CROSS, 7, 0, 0), (BEGIN, 7, 0, 2), (DOWN, 1, 0, 0), (CROSS, 6, 0, 1),
+     (CROSS, 5, 0, 1),),
+    ((DOWN, 1, 0, 1), (ALONG, 5, 0, -1), (ALONG, 5, 0, 0), (ALONG, 5, 0, 1), (FACE, 4, 2, -1), (FACE, 4, 2, 0),
+     (ALONG, 6, 2, 0), (ALONG, 4, 3, -1), (ALONG, 4, 3, 0), (ALONG, 4, 3, 1), (FACE, 3, 3, -1),
+     (FACE, 3, 3, 0), (ALONG, 5, 2, 1), (ALONG, 7, 2, -1),),
+    ((ACROSS, 5, 0, -1), (ACROSS, 5, 0, 0), (UP, 0, 0, 0), (DOWN, 0, 0, 0), (ALONG, 6, 0, -1), (ALONG, 6, 0, 0),
+     (ALONG, 6, 0, 1), (FACE, 4, 3, -1), (FACE, 4, 3, 0), (CROSS, 7, 0, 1), (ALONG, 5, 3, -1), (ALONG, 5, 3, 0),
+     (ALONG, 5, 3, 1), (CROSS, 6, 0, 2), (BEGIN, 7, 0, 1), (UP, 0, 0, 1), (DOWN, 0, 0, 1), (ALONG, 6, 2, 1),
+     (ALONG, 7, 2, 0), (FACE, 5, 2, -1), (FACE, 5, 2, 0), (ALONG, 6, 3, -1), (ALONG, 6, 3, 0), (ALONG, 7, 0, -1),
+     (ALONG, 7, 0, 0), (ALONG, 7, 0, 1), (UP, 2, 0, 0), (FACE, 5, 3, -1), (FACE, 5, 3, 0), (DOWN, 2, 0, 0),
+     (CROSS, 7, 0, 2), (ALONG, 6, 3, 1), (ACROSS, 6, 0, -1), (ACROSS, 6, 0, 0), (UP, 2, 0, 1), (DOWN, 2, 0, 1),
+     (UP, 3, 0, 0), (ALONG, 7, 2, 1), (FACE, 6, 2, -1), (FACE, 6, 2, 0), (ALONG, 7, 3, -1), (ALONG, 7, 3, 0),
+     (UP, 3, 0, 1), (DOWN, 3, 0, 1), (DOWN, 3, 0, 0), (FACE, 6, 3, -1), (FACE, 6, 3, 0), (ALONG, 7, 3, 1),
      ),
-    ((FACE, 4, 2, -1), (FACE, 4, 2, 0), (ALONG, 5, 1, -1), (ALONG, 5, 1, 0), (ALONG, 5, 1, 1), (CROSS, 6, 0, -1),
-     (CROSS, 6, 0, 0), (CROSS, 6, 0, 1), (ALONG, 5, 2, -1), (ALONG, 5, 2, 0), (ALONG, 5, 2, 1),
-     (FACE, 1, 3, -1), (FACE, 1, 3, 0), (ALONG, 3, 3, -1), (ALONG, 3, 3, 0), (ALONG, 3, 3, 1), (CROSS, 7, 0, -1),
-     (CROSS, 7, 0, 1), (DOWN, 0, 0, 0), (UP, 0, 0, 0), (CROSS, 7, 0, 0),),
-    ((FACE, 2, 3, -1), (FACE, 2, 3, 0), (ALONG, 6, 1, -1), (ALONG, 6, 1, 0), (FACE, 3, 3, -1), (FACE, 3, 3, 0),
-     (FACE, 5, 1, -1), (FACE, 5, 1, 0), (DOWN, 1, 0, 0), (UP, 1, 0, 0),),
-    ((ALONG, 6, 2, -1), (ALONG, 6, 2, 0), (FACE, 5, 2, -1), (FACE, 5, 2, 0), (SETTLE, 3, 3, -1),
-     (SETTLE, 3, 3, 0), (DOWN, 2, 0, 0), (UP, 2, 0, 0), (ALONG, 4, 3, -1), (ALONG, 4, 3, 0), (SETTLE, 5, 1, -1),
-     (SETTLE, 5, 1, 0), (FACE, 6, 1, -1), (FACE, 6, 1, 0), (ALONG, 5, 3, -1), (ALONG, 5, 3, 0),
-     (ALONG, 5, 3, 1),),
-    ((DOWN, 3, 0, 0), (UP, 3, 0, 0), (SETTLE, 5, 2, -1), (SETTLE, 5, 2, 0), (FACE, 6, 2, -1), (FACE, 6, 2, 0),
-     (ALONG, 7, 1, -1), (ALONG, 7, 1, 0), (FACE, 4, 3, -1), (FACE, 4, 3, 0), (ALONG, 7, 2, -1),
-     (ALONG, 7, 2, 0), (FACE, 5, 3, -1), (FACE, 5, 3, 0),),
-    ((DOWN, 4, 0, 0), (UP, 4, 0, 0), (FACE, 7, 1, -1), (FACE, 7, 1, 0), (ALONG, 6, 3, -1), (ALONG, 6, 3, 0),
-     (SETTLE, 5, 3, -1), (SETTLE, 5, 3, 0), (FACE, 7, 2, -1), (FACE, 7, 2, 0),),
-    ((DOWN, 5, 0, 0), (UP, 5, 0, 0), (FACE, 6, 3, -1), (FACE, 6, 3, 0), (ALONG, 7, 3, -1), (ALONG, 7, 3, 0),
+    ((UP, 4, 0, 0),),
+    ((DOWN, 5, 0, 0), (UP, 5, 0, 0), (UP, 5, 0, 1), (ACROSS, 7, 0, -1), (ACROSS, 7, 0, 0), (DOWN, 5, 0, 1),
      ),
-    ((DOWN, 6, 0, 0), (UP, 6, 0, 0), (FACE, 7, 3, -1), (FACE, 7, 3, 0),),
-    ((DOWN, 7, 0, 0), (UP, 7, 0, 0),),
+    ((DOWN, 4, 0, 1), (UP, 4, 0, 1), (DOWN, 4, 0, 0), (FACE, 7, 3, -1), (FACE, 7, 3, 0), (FACE, 7, 2, -1),
+     (FACE, 7, 2, 0), (RELAY, 1, 0, 0), (DOWN, 6, 0, 0),),
+    ((UP, 6, 0, 1), (DOWN, 6, 0, 1), (UP, 6, 0, 0), (DOWN, 7, 0, 0), (UP, 7, 0, 0), (DOWN, 7, 0, 1),
+     (RELAY, 5, 0, 0), (UP, 7, 0, 1),),
 )
-INNER = (
-    ((BEGIN, 0, 0, 0), (BEGIN, 0, 0, 1), (BEGIN, 0, 0, 2), (BEGIN, 1, 0, 0), (BEGIN, 1, 0, 1), (BEGIN, 1, 0, 2),
-     (BEGIN, 2, 0, 0), (BEGIN, 2, 0, 1), (BEGIN, 2, 0, 2),),
-    (),
-    (),
-    ((BEGIN, 3, 0, 0),),
+INNER_SECOND = (
+    ((BEGIN, 0, 0, 0), (BEGIN, 0, 0, 1), (BEGIN, 0, 0, 2), (BEGIN, 1, 0, 0),),
+    ((BEGIN, 1, 0, 1), (BEGIN, 1, 0, 2),),
+    (),
+    ((BEGIN, 2, 0, 0),),
+    ((BEGIN, 2, 0, 2),),
+    (),
+    (),
+    ((BEGIN, 2, 0, 1),),
+    (),
     ((BEGIN, 3, 0, 1),),
-    ((BEGIN, 4, 0, 0),),
-    (),
-    ((CROSS, 0, 0, -1), (CROSS, 0, 0, 0), (CROSS, 0, 0, 1), (BEGIN, 5, 0, 0), (BEGIN, 3, 0, 2),
-     ),
-    (),
-    ((BEGIN, 6, 0, 0), (CROSS, 1, 0, -1), (CROSS, 1, 0, 0), (CROSS, 1, 0, 1), (CROSS, 1, 0, 2),
-     ),
-    ((BEGIN, 7, 0, 0),),
-    ((CROSS, 2, 0, -1), (CROSS, 2, 0, 0), (CROSS, 2, 0, 1), (CROSS, 2, 0, 2),),
-    ((BEGIN, 4, 0, 2),),
-    ((ACROSS, 0, 0, -1), (ACROSS, 0, 0, 0), (CROSS, 3, 0, -1), (CROSS, 3, 0, 0), (CROSS, 3, 0, 1),
-     ),
-    ((ALONG, 0, 2, -1), (ALONG, 0, 2, 0), (ALONG, 0, 2, 1),),
-    ((ACROSS, 1, 0, -1), (ACROSS, 1, 0, 0), (BEGIN, 4, 0, 1),),
-    ((CROSS, 4, 0, -1),),
-    ((ALONG, 1, 2, -1), (ALONG, 1, 2, 0), (ALONG, 1, 2, 1),),
-    ((ACROSS, 2, 0, -1), (ACROSS, 2, 0, 0), (CROSS, 5, 0, -1),),
-    ((CROSS, 4, 0, 0), (ALONG, 0, 0, -1), (ALONG, 0, 0, 0), (ALONG, 0, 0, 1), (ALONG, 2, 2, -1),
-     (ALONG, 2, 2, 0), (ALONG, 2, 2, 1),),
-    ((BEGIN, 5, 0, 2), (ACROSS, 3, 0, -1), (ACROSS, 3, 0, 0), (CROSS, 6, 0, -1), (CROSS, 7, 0, -1),
-     (BEGIN, 6, 0, 2), (ALONG, 3, 2, -1), (ALONG, 3, 2, 0), (FACE, 0, 2, -1), (FACE, 0, 2, 0), (CROSS, 4, 0, 1),
-     (BEGIN, 5, 0, 1), (ALONG, 3, 2, 1), (BEGIN, 7, 0, 2), (ALONG, 1, 0, -1), (ALONG, 1, 0, 0),
-     (ALONG, 1, 0, 1), (ALONG, 0, 3, -1), (ALONG, 0, 3, 0), (ALONG, 0, 3, 1), (FACE, 1, 2, -1),
-     (FACE, 1, 2, 0), (BEGIN, 6, 0, 1), (ALONG, 2, 0, -1), (ALONG, 2, 0, 0), (ALONG, 2, 0, 1), (CROSS, 5, 0, 0),
-     (ALONG, 4, 2, -1), (ALONG, 4, 2, 0), (FACE, 2, 2, -1), (FACE, 2, 2, 0), (CROSS, 4, 0, 2), (ALONG, 1, 3, -1),
-     (ALONG, 1, 3, 0), (ALONG, 1, 3, 1), (FACE, 0, 3, -1), (FACE, 0, 3, 0), (BEGIN, 7, 0, 1),),
-    ((CROSS, 6, 0, 0), (ALONG, 4, 2, 1), (ALONG, 3, 0, -1), (ALONG, 3, 0, 0), (ALONG, 3, 0, 1),
-     (ALONG, 2, 3, -1), (ALONG, 2, 3, 0), (ALONG, 2, 3, 1), (FACE, 3, 2, -1), (FACE, 3, 2, 0), (ALONG, 5, 2, -1),
-     (ALONG, 5, 2, 0), (FACE, 1, 3, -1), (FACE, 1, 3, 0), (ACROSS, 4, 0, -1), (ACROSS, 4, 0, 0),
-     ),
-    ((UP, 1, 0, 0), (DOWN, 1, 0, 0), (CROSS, 6, 0, 1), (CROSS, 7, 0, 0), (CROSS, 5, 0, 1), (UP, 0, 0, 0),
-     (DOWN, 0, 0, 0), (ALONG, 4, 0, -1), (ALONG, 4, 0, 0), (ALONG, 4, 0, 1), (ALONG, 3, 3, -1),
-     (ALONG, 3, 3, 0), (ALONG, 3, 3, 1), (FACE, 2, 3, -1), (FACE, 2, 3, 0), (ALONG, 5, 2, 1), (ALONG, 6, 2, -1),
-     (ALONG, 6, 2, 0),),
-    ((FACE, 4, 2, -1), (FACE, 4, 2, 0), (ALONG, 5, 0, -1), (ALONG, 5, 0, 0), (ALONG, 5, 0, 1), (ALONG, 4, 3, -1),
-     (ALONG, 4, 3, 0), (ALONG, 4, 3, 1), (FACE, 3, 3, -1), (FACE, 3, 3, 0), (ALONG, 7, 2, -1), (UP, 2, 0, 0),
-     (DOWN, 2, 0, 0), (ACROSS, 5, 0, -1), (ACROSS, 5, 0, 0), (CROSS, 7, 0, 1),),
-    ((CROSS, 6, 0, 2), (ALONG, 7, 2, 0), (ALONG, 6, 0, -1), (ALONG, 6, 0, 0), (ALONG, 6, 0, 1),
-     (ALONG, 5, 3, -1), (ALONG, 5, 3, 0), (ALONG, 5, 3, 1), (ALONG, 6, 2, 1), (FACE, 5, 2, -1),
-     (FACE, 5, 2, 0), (UP, 3, 0, 0), (DOWN, 3, 0, 0), (FACE, 4, 3, -1), (FACE, 4, 3, 0),),
-    ((CROSS, 7, 0, 2), (ALONG, 6, 3, -1), (ALONG, 6, 3, 0), (ALONG, 6, 3, 1), (RELAY, 1, 0, 0),
-     (UP, 4, 0, 0), (DOWN, 4, 0, 0), (ALONG, 7, 0, -1), (ALONG, 7, 0, 0), (ALONG, 7, 0, 1), (FACE, 5, 3, -1),
-     (FACE, 5, 3, 0), (ACROSS, 6, 0, -1), (ACROSS, 6, 0, 0), (ALONG, 7, 2, 1),),
-    ((DOWN, 5, 0, 0), (UP, 5, 0, 0), (FACE, 6, 2, -1), (FACE, 6, 2, 0), (FACE, 6, 3, -1), (FACE, 6, 3, 0),
-     (ALONG, 7, 3, -1), (ALONG, 7, 3, 0), (ALONG, 7, 3, 1), (ACROSS, 7, 0, -1), (ACROSS, 7, 0, 0),
-     ),
-    ((DOWN, 6, 0, 0), (UP, 6, 0, 0), (FACE, 7, 2, -1), (FACE, 7, 2, 0), (FACE, 7, 3, -1), (FACE, 7, 3, 0),
-     ),
-    ((DOWN, 7, 0, 0), (UP, 7, 0, 0), (RELAY, 5, 0, 0),),
+    (),
+    ((BEGIN, 3, 0, 0), (BEGIN, 4, 0, 0),),
+    ((CROSS, 0, 0, -1), (CROSS, 0, 0, 0), (CROSS, 0, 0, 1),),
+    (),
+    (),
+    (),
+    ((CROSS, 1, 0, -1), (CROSS, 1, 0, 0), (CROSS, 1, 0, 1), (CROSS, 1, 0, 2),),
+    (),
+    (),
+    ((BEGIN, 5, 0, 0),),
+    ((CROSS, 2, 0, -1), (CROSS, 2, 0, 0), (CROSS, 2, 0, 2), (CROSS, 2, 0, 1), (BEGIN, 3, 0, 2),
+     (CROSS, 3, 0, -1), (CROSS, 3, 0, 1), (ALONG, 0, 2, -1), (ALONG, 0, 2, 0), (ALONG, 0, 2, 1),
+     (CROSS, 3, 0, 0), (ACROSS, 0, 0, -1), (ACROSS, 0, 0, 0), (BEGIN, 7, 0, 0), (CROSS, 4, 0, -1),
+     (ALONG, 1, 2, -1), (ALONG, 1, 2, 0), (ALONG, 1, 2, 1), (ALONG, 2, 2, -1), (CROSS, 5, 0, -1),
+     (ALONG, 0, 0, -1), (ALONG, 0, 0, 0), (ALONG, 0, 0, 1), (ALONG, 2, 2, 0), (ACROSS, 1, 0, -1),
+     (ACROSS, 1, 0, 0), (ACROSS, 2, 0, -1), (ACROSS, 2, 0, 0), (BEGIN, 6, 0, 0), (CROSS, 6, 0, -1),
+     (ALONG, 3, 2, -1), (ALONG, 2, 2, 1), (FACE, 0, 2, -1), (FACE, 0, 2, 0), (ALONG, 1, 0, -1),
+     (ALONG, 1, 0, 0), (ALONG, 1, 0, 1), (CROSS, 7, 0, -1), (ACROSS, 3, 0, -1), (ACROSS, 3, 0, 0),
+     (ALONG, 3, 2, 0), (BEGIN, 4, 0, 2), (ALONG, 0, 3, -1), (ALONG, 0, 3, 0), (BEGIN, 4, 0, 1),
+     (ALONG, 0, 3, 1), (CROSS, 4, 0, 0), (FACE, 1, 2, -1), (FACE, 1, 2, 0), (ALONG, 2, 0, -1), (ALONG, 2, 0, 0),
+     (ALONG, 2, 0, 1), (CROSS, 4, 0, 1), (ALONG, 1, 3, -1), (ALONG, 1, 3, 0), (FACE, 2, 2, -1),
+     (FACE, 2, 2, 0), (ALONG, 1, 3, 1), (ALONG, 3, 2, 1), (BEGIN, 5, 0, 2), (ALONG, 4, 2, -1), (FACE, 0, 3, -1),
+     (FACE, 0, 3, 0), (ALONG, 4, 2, 0), (CROSS, 5, 0, 0), (CROSS, 4, 0, 2), (BEGIN, 6, 0, 2), (ALONG, 3, 0, -1),
+     (ALONG, 3, 0, 0), (ALONG, 3, 0, 1), (ALONG, 2, 3, -1), (ALONG, 2, 3, 0), (ALONG, 2, 3, 1),
+     (FACE, 1, 3, -1), (FACE, 1, 3, 0), (ALONG, 4, 2, 1), (BEGIN, 5, 0, 1),),
+    ((ALONG, 5, 2, -1), (FACE, 3, 2, -1), (FACE, 3, 2, 0), (CROSS, 6, 0, 0), (ALONG, 5, 2, 0), (DOWN, 0, 0, 0),
+     (BEGIN, 6, 0, 1), (ALONG, 4, 0, -1), (ALONG, 4, 0, 0), (ALONG, 4, 0, 1),),
+    ((ALONG, 3, 3, -1), (ALONG, 3, 3, 0), (ALONG, 3, 3, 1), (FACE, 2, 3, -1), (FACE, 2, 3, 0), (ACROSS, 4, 0, -1),
+     (ACROSS, 4, 0, 0), (BEGIN, 7, 0, 2), (UP, 0, 0, 0), (CROSS, 5, 0, 1), (ALONG, 6, 2, -1), (CROSS, 6, 0, 1),
+     (CROSS, 7, 0, 0),),
+    ((DOWN, 0, 0, 1), (FACE, 4, 2, -1), (FACE, 4, 2, 0), (ALONG, 5, 0, -1), (ALONG, 5, 0, 0), (ALONG, 5, 0, 1),
+     (ALONG, 4, 3, -1), (ALONG, 4, 3, 0), (ALONG, 4, 3, 1), (RELAY, 1, 0, 0), (DOWN, 1, 0, 0), (ALONG, 5, 2, 1),
+     (UP, 0, 0, 1), (FACE, 3, 3, -1), (FACE, 3, 3, 0), (UP, 1, 0, 0), (UP, 1, 0, 1), (ALONG, 6, 2, 0),
+     (ALONG, 7, 2, -1), (DOWN, 1, 0, 1),),
+    ((UP, 2, 0, 0), (ALONG, 6, 0, -1), (ALONG, 6, 0, 0), (ALONG, 6, 0, 1), (DOWN, 2, 0, 0), (ALONG, 5, 3, -1),
+     (ALONG, 5, 3, 0), (CROSS, 7, 0, 1), (ACROSS, 5, 0, -1), (ACROSS, 5, 0, 0), (FACE, 4, 3, -1),
+     (FACE, 4, 3, 0), (ALONG, 5, 3, 1), (BEGIN, 7, 0, 1),),
+    ((UP, 2, 0, 1), (ALONG, 6, 2, 1), (CROSS, 6, 0, 2), (DOWN, 2, 0, 1), (DOWN, 4, 0, 0), (FACE, 5, 2, -1),
+     (FACE, 5, 2, 0), (DOWN, 3, 0, 1), (UP, 3, 0, 1), (UP, 3, 0, 0), (ALONG, 6, 3, -1), (ALONG, 6, 3, 0),
+     (ALONG, 7, 0, -1), (ALONG, 7, 0, 0), (ALONG, 7, 0, 1), (FACE, 5, 3, -1), (FACE, 5, 3, 0), (ALONG, 7, 2, 0),
+     (UP, 4, 0, 0), (ALONG, 6, 3, 1), (DOWN, 3, 0, 0), (ACROSS, 6, 0, -1), (ACROSS, 6, 0, 0), (ALONG, 7, 2, 1),
+     (CROSS, 7, 0, 2), (UP, 4, 0, 1), (DOWN, 4, 0, 1), (FACE, 6, 2, -1), (FACE, 6, 2, 0), (FACE, 6, 3, -1),
+     (FACE, 6, 3, 0), (ALONG, 7, 3, -1), (ALONG, 7, 3, 0), (ACROSS, 7, 0, -1), (ACROSS, 7, 0, 0),
+     (FACE, 7, 2, -1), (FACE, 7, 2, 0), (ALONG, 7, 3, 1),),
+    ((DOWN, 5, 0, 0), (DOWN, 5, 0, 1), (UP, 5, 0, 0), (UP, 5, 0, 1),),
+    ((UP, 6, 0, 0), (RELAY, 5, 0, 0), (UP, 6, 0, 1), (DOWN, 6, 0, 1), (FACE, 7, 3, -1), (FACE, 7, 3, 0),
+     (DOWN, 6, 0, 0),),
+    ((DOWN, 7, 0, 0), (UP, 7, 0, 0), (DOWN, 7, 0, 1), (UP, 7, 0, 1),),
 )
 
 
 class Work:
     def __init__(self, n, refs, me):
-        (self.gain, self.lengths, self.pages, self.freq, self.wide_gain, self.xbuf, self.onehot,
-         self.cosine, self.sine) = refs
+        (self.gain, self.lengths, self.pages, self.freq, self.wide_gain, self.xbuf, self.raw, self.found,
+         self.page_of, self.found_sem, self.cosine, self.sine) = refs
         self.n, self.me = n, me
         self.tok_rows, self.features = self.xbuf.shape
         self.length_each = self.tok_rows * n // 2
@@ -172,31 +304,17 @@
 
         lax.fori_loop(0, rows_here // 32, body, 0)
 
-    def mark_rows(self):
-        tok_rows = self.tok_rows
-        second_prompt = (self.me * tok_rows) // self.length_each
-        limit = self.lengths[0] + second_prompt * (self.lengths[1] - self.lengths[0])
-        page_count = tok_rows // PAGE
-        token = lax.broadcasted_iota(jnp.int32, (page_count, tok_rows), 1)
-        page = lax.broadcasted_iota(jnp.int32, (page_count, tok_rows), 0)
-        used = jnp.where((token // PAGE == page) & (self.first + token < limit), 1.0, 0.0)
-        used = used.astype(jnp.bfloat16)
-        slot = lax.rem(self.pages[...], SLOTS)
-
-        def hot(i, carry):
-            at = i * BLOCK
-            row = lax.broadcasted_iota(jnp.int32, (BLOCK, page_count), 0) + at
-            held = jnp.where(row // PAGE == slot, 1.0, 0.0).astype(jnp.bfloat16)
-            spread = jnp.dot(held, used, preferred_element_type=jnp.float32)
-            row = lax.broadcasted_iota(jnp.int32, (BLOCK, tok_rows), 0)
-            column = lax.broadcasted_iota(jnp.int32, (BLOCK, tok_rows), 1)
-            same = lax.rem(row, PAGE) == lax.rem(column, PAGE)
-            self.onehot[pl.ds(pl.multiple_of(at, BLOCK), BLOCK), :] = jnp.where(
-                same, spread, 0.0
-            ).astype(jnp.bfloat16)
-            return carry
-
-        lax.fori_loop(0, REGIONS, hot, 0)
+    def find_pages(self):
+        page_count = self.tok_rows // PAGE
+        lane = lax.broadcasted_iota(jnp.int32, self.found.shape, 1)
+        page_of = jnp.full(self.found.shape, page_count, jnp.int32)
+        for page in range(page_count):
+            page_of = jnp.where(lane == lax.rem(self.pages[page], SLOTS), page, page_of)
+        self.found[...] = page_of
+        self.raw[page_count] = jnp.zeros(self.raw.shape[1:], jnp.bfloat16)
+        copy = pltpu.make_async_copy(self.found, self.page_of, self.found_sem)
+        copy.start()
+        copy.wait()
 
     def angles(self, at, rows_here):
         def turn(i, carry):
@@ -212,15 +330,27 @@
         lax.fori_loop(0, rows_here // 64, turn, 0)
 
     def project(self, weights, is_key, put):
-        raw = jnp.dot(self.xbuf[...], weights, preferred_element_type=jnp.float32)
+        part = self.tok_rows // 2
+        raw = [
+            jnp.dot(self.xbuf[i * part : (i + 1) * part, :], weights, preferred_element_type=jnp.float32)
+            for i in range(2)
+        ]
+        raw = jnp.concatenate(raw, axis=0)
         if is_key:
             heads = []
             for head in range(weights.shape[1] // HEAD):
                 one = raw[:, head * HEAD : (head + 1) * HEAD]
                 heads.append(one * self.cosine[...] + pltpu.roll(one, HEAD // 2, 1) * self.sine[...])
             raw = jnp.concatenate(heads, axis=1)
-        placed = jnp.dot(self.onehot[...], raw.astype(jnp.bfloat16), preferred_element_type=jnp.float32)
-        put(placed.astype(jnp.bfloat16))
+        second_prompt = (self.me * self.tok_rows) // self.length_each
+        limit = self.lengths[0] + second_prompt * (self.lengths[1] - self.lengths[0])
+        row = lax.broadcasted_iota(jnp.int32, raw.shape, 0)
+        raw = jnp.where(self.first + row < limit, raw, 0.0)
+        wide = weights.shape[1]
+        raw = raw.astype(jnp.bfloat16).reshape(self.tok_rows // PAGE, PAGE, wide)
+        self.raw[0 : self.tok_rows // PAGE, :, 0:wide] = raw
+        for slot in range(SLOTS):
+            put(slot * PAGE, self.raw[self.page_of[0, slot]][:, 0:wide])
 
 
 def copy_to(ref, send_sem, recv_sem, group_at, seq_at, dst=None):
@@ -240,7 +370,7 @@
 
 def line_kernel(
     n, tokens, gain, w_key, w_value, lengths, pages, freq, out,
-    wide_gain, wbuf, xbuf, pbuf, rbuf, onehot, cosine, sine,
+    wide_gain, wbuf, xbuf, pbuf, rbuf, raw, found, page_of, found_sem, cosine, sine,
     load_sem, tok_sem, ys, yr, fr, fq, zi, zo, zr, xs, xo, xr, xq, cs, cr, hs, hr, rs, rr,
 ):
     chunks, depth = wbuf.shape[0], wbuf.shape[1]
@@ -446,8 +576,10 @@
                 src, dst = spot(g, region)
                 copy_to(src, hs.at[g, region], hr.at[g, region], group, to_core, dst)
 
-    def pages_off_chip(g, way):
-        page_to(g, 4 if way == UP else 0)
+    def pages_off_chip(g, way, which):
+        if which == 0:
+            page_to(g, 4 if way == UP else 0)
+            return
 
         @pl.when(core == (1 if way == UP else 0))
         def _():
@@ -472,7 +604,7 @@
     def run(steps, waits, sends, seen):
         for what, j, k, which in steps:
             if what in (UP, DOWN):
-                pages_off_chip(j, what)
+                pages_off_chip(j, what, which)
             elif what == RELAY:
                 pass_pages(j)
             elif what == BEGIN:
@@ -486,7 +618,7 @@
             else:
                 sends(j, what, k)[which]()
 
-    work = Work(n, (gain, lengths, pages, freq, wide_gain, xbuf, onehot, cosine, sine), me)
+    work = Work(n, (gain, lengths, pages, freq, wide_gain, xbuf, raw, found, page_of, found_sem, cosine, sine), me)
     tok_rows = work.tok_rows
 
     def project(g):
@@ -497,8 +629,8 @@
             blocks.append(wbuf[j].reshape(work.features, width))
         weights = blocks[0] if len(blocks) == 1 else jnp.concatenate(blocks, axis=1)
 
-        def put(placed):
-            pbuf[g, :, 0:wide] = placed
+        def put(at_row, page):
+            pbuf[g, at_row : at_row + PAGE, 0:wide] = page
 
         work.project(weights, at_chunk < per_kind, put)
         pages_on_chip(g)
@@ -506,27 +638,29 @@
     sixteenth = tok_rows // 16
     jobs = [lambda: (work.spread_gain(), token_copy.wait())]
     jobs += [functools.partial(work.normalise, i * sixteenth, sixteenth) for i in range(16)]
-    jobs += [work.mark_rows]
+    jobs += [work.find_pages]
     jobs += [functools.partial(work.angles, i * (tok_rows // 2), tok_rows // 2) for i in range(2)]
     jobs, projects = iter(jobs), iter(range(len(GROUPS)))
-    seen_end, seen_inner = set(), set()
+    inner, second = jnp.logical_not(is_end), y != high
+    first = jnp.logical_not(second)
+    kinds = (
+        (is_end & first, END_FIRST, end_waits, end_sends, set()),
+        (is_end & second, END_SECOND, end_waits, end_sends, set()),
+        (inner & first, INNER_FIRST, inner_waits, inner_sends, set()),
+        (inner & second, INNER_SECOND, inner_waits, inner_sends, set()),
+    )
     for stretch in range(len(COMPUTE) + 1):
         if stretch:
             if COMPUTE[stretch - 1]:
                 project(next(projects))
             else:
                 next(jobs)()
-        if END[stretch]:
-
-            @pl.when(is_end)
-            def _():
-                run(END[stretch], end_waits, end_sends, seen_end)
-
-        if INNER[stretch]:
-
-            @pl.when(jnp.logical_not(is_end))
-            def _():
-                run(INNER[stretch], inner_waits, inner_sends, seen_inner)
+        for here, steps, waits, sends, seen in kinds:
+            if steps[stretch]:
+
+                @pl.when(here)
+                def _():
+                    run(steps[stretch], waits, sends, seen)
 
     def count(pieces, sem):
         wait(xbuf.at[pl.ds(0, half), pl.ds(0, pieces * width)], sem)
@@ -569,7 +703,7 @@
 
 def loop_kernel(
     n, tokens, gain, w_key, w_value, lengths, pages, freq, out,
-    wide_gain, wbuf, xbuf, pbuf, onehot, cosine, sine,
+    wide_gain, wbuf, xbuf, pbuf, raw, found, page_of, found_sem, cosine, sine,
     load_sem, tok_sem, ys, yr, zs, zr, xs, xr, cs, cr, hs, hr,
 ):
     chunks, depth = wbuf.shape[0], wbuf.shape[1]
@@ -674,13 +808,13 @@
 
         both(k, visit)
 
-    work = Work(n, (gain, lengths, pages, freq, wide_gain, xbuf, onehot, cosine, sine), me)
+    work = Work(n, (gain, lengths, pages, freq, wide_gain, xbuf, raw, found, page_of, found_sem, cosine, sine), me)
 
     def project(j):
         wait(wbuf.at[j, :, :, other_core], cr.at[j])
         for at in range(0, width, TILE):
-            def put(placed):
-                pbuf[j, :, at : at + TILE] = placed
+            def put(at_row, page):
+                pbuf[j, at_row : at_row + PAGE, at : at + TILE] = page
 
             weights = wbuf[j, :, :, :, :, :, at : at + TILE].reshape(work.features, TILE)
             work.project(weights, j < per_kind, put)
@@ -706,7 +840,7 @@
     work.spread_gain()
     token_copy.wait()
     work.normalise(0, work.tok_rows)
-    work.mark_rows()
+    work.find_pages()
     work.angles(0, work.tok_rows)
     for j in range(chunks):
         cross(j)
@@ -765,7 +899,10 @@
     if in_line:
         scratch.append(pltpu.VMEM((max(len(RELAYED), 1), 2, BLOCK, wide), jnp.bfloat16))
     scratch += [
-        pltpu.VMEM((ROWS, tok_rows), jnp.bfloat16),
+        pltpu.VMEM((tok_rows // PAGE + 1, PAGE, TILE), jnp.bfloat16),
+        pltpu.VMEM((1, HEAD), jnp.int32),
+        pltpu.SMEM((1, HEAD), jnp.int32),
+        dma,
         pltpu.VMEM((tok_rows, HEAD), jnp.float32),
         pltpu.VMEM((tok_rows, HEAD), jnp.float32),
         dma((chunks, 2)),
@@ -782,14 +919,14 @@
                     by_region, by_region]
     cache = pl.pallas_call(
         functools.partial(line_kernel if in_line else loop_kernel, n),
-        out_shape=jax.ShapeDtypeStruct((2, ROWS, columns), jnp.bfloat16),
-        in_specs=[hbm, vmem, hbm, hbm, smem, vmem, vmem],
-        out_specs=hbm,
+        out_shape=pltpu.VMEM((2, ROWS, columns), jnp.bfloat16),
+        in_specs=[hbm, vmem, hbm, hbm, smem, smem, vmem],
+        out_specs=vmem,
         scratch_shapes=scratch,
         compiler_params=pltpu.CompilerParams(
             collective_id=0, has_side_effects=True, vmem_limit_bytes=60 * 2**20
         ),
-    )(tokens, norm_gain.reshape(-1, HEAD), w_key, w_value, lengths, page_table[None, :], freq)
+    )(tokens, norm_gain.reshape(-1, HEAD), w_key, w_value, lengths, page_table, freq)
     return cache.reshape(2, SLOTS, PAGE, columns)
 
 

time: 101 us -> 90.1 us (0.89)
  Pallas kernels: 97.5 us -> 88.5 us
  local copies, waits for them, and re-layouts: 3.67 us -> 1.49 us
    pallas_call x1, Pallas kernels: 97.5 us -> 88.5 us  [on_device(): pl.pallas_call(functools.partial(line_kernel if in_line else loop_kernel,...]
    unnamed x1, local copies, waits for them, and re-layouts: 3.67 us -> 1.49 us
where the time goes in v2:
time: 90.1 us; the launch traced here: 90 us
  Pallas kernels  88.5 us (98%)
  local copies, waits for them, and re-layouts  1.49 us (2%)
    pallas_call x1, Pallas kernels, on_device(): pl.pallas_call(functools.partial(line_kernel if in_line else loop_kernel,...  88.5 us

profile of v2, /device:TPU:1, one launch (start us, length us, event | category | flops | bytes accessed | tf_op | source)
XLA Modules:
  0.0 90.0 jit_solution(7884405836882222584)
XLA Ops:
  0.0 88.5 %shard_map.73 = bf16[2,640,1024]{2,1,0:T(8,128)(2,1)S(1)} custom-call(bf16[512,4096]{1,0:T(8,128)(2,1)} %tokens.1, bf16[32,128]{1,0:T(8,128)(2,1)} %bitcast.3, bf16[256,1024]{1,0:T(8,128)(2,1)} %w_key.1, bf16[256,1024]{1,0:T(8,128)(2,1)} %w_value.1, s32[2]{0:T(128)} %lengths.1, s32[32]{0:T(128)} %pages.1, f32[1,128]{1,0:T(1,128)} %constant.2.clone.freq), custom_call_target="tpu_custom_call" | custom-call | tf_op jit(solution)/shard_map/pallas_call | solution.py:920
  88.6 1.5 %copy.9 = bf16[2,40,16,1024]{3,2,1,0:T(8,128)(2,1)} copy(bf16[2,40,16,1024]{3,2,1,0:T(8,128)(2,1)S(1)} %bitcast.2) | data formatting | bytes 5242880

commit v3 on v2

--- a/solution.py
+++ b/solution.py
@@ -329,13 +329,23 @@
 
         lax.fori_loop(0, rows_here // 64, turn, 0)
 
-    def project(self, weights, is_key, put):
+    def project(self, blocks, is_key, put):
         part = self.tok_rows // 2
-        raw = [
-            jnp.dot(self.xbuf[i * part : (i + 1) * part, :], weights, preferred_element_type=jnp.float32)
-            for i in range(2)
-        ]
-        raw = jnp.concatenate(raw, axis=0)
+        raw = None
+        for ready, at, load in blocks:
+            ready()
+            weights = load()
+            features = pl.ds(at, weights.shape[0])
+            halves = [
+                jnp.dot(
+                    self.xbuf[i * part : (i + 1) * part, features],
+                    weights,
+                    preferred_element_type=jnp.float32,
+                )
+                for i in range(2)
+            ]
+            product = jnp.concatenate(halves, axis=0)
+            raw = product if raw is None else raw + product
         if is_key:
             heads = []
             for head in range(weights.shape[1] // HEAD):
@@ -371,7 +381,7 @@
 def line_kernel(
     n, tokens, gain, w_key, w_value, lengths, pages, freq, out,
     wide_gain, wbuf, xbuf, pbuf, rbuf, raw, found, page_of, found_sem, cosine, sine,
-    load_sem, tok_sem, ys, yr, fr, fq, zi, zo, zr, xs, xo, xr, xq, cs, cr, hs, hr, rs, rr,
+    load_sem, tok_sem, ys, yr, fr, fq, zi, zo, zr, xs, xo, xr, xq, cs, cr, cl, hs, hr, rs, rr,
 ):
     chunks, depth = wbuf.shape[0], wbuf.shape[1]
     half, width = wbuf.shape[5], wbuf.shape[6]
@@ -414,22 +424,21 @@
             for part in range(2)
         ]
 
+    barrier = pltpu.get_barrier_semaphore()
+
+    def greet(group_at, seq_at):
+        pl.semaphore_signal(
+            barrier, inc=1, device_id={"group": group_at, "seq": seq_at}, device_id_type=MESH
+        )
+
+    greet(other_group, me)
+    for step in range(1, n):
+        greet(group, lax.rem(me + step, n))
     for j in range(chunks):
         for copy in load(j):
             copy.start()
     token_copy = pltpu.make_async_copy(tokens, xbuf, tok_sem)
     token_copy.start()
-
-    barrier = pltpu.get_barrier_semaphore()
-
-    def greet(group_at, seq_at):
-        pl.semaphore_signal(
-            barrier, inc=1, device_id={"group": group_at, "seq": seq_at}, device_id_type=MESH
-        )
-
-    greet(other_group, me)
-    for step in range(1, n):
-        greet(group, lax.rem(me + step, n))
     pl.semaphore_wait(barrier, n)
 
     def over_y(ref, j, sem):
@@ -444,8 +453,8 @@
     def outward(ref, j, zz):
         copy_to(ref, zo.at[j], zr.at[j, zz], group, seq_of(at(0), y, core))
 
-    def to_partner(j, zz):
-        copy_to(layer(j, zz), cs.at[j], cr.at[j], group, to_core)
+    def to_partner(j, zz, p=0):
+        copy_to(layer(j, zz), cs.at[j], (cl if p == LAYERS - 1 else cr).at[j], group, to_core)
 
     def loaded(j):
         for copy in load(j):
@@ -473,7 +482,7 @@
     def end_sends(j, what, k):
         form, both = CHUNKS[j]
         zz = at(k)
-        partner = functools.partial(to_partner, j, zz)
+        partner = functools.partial(to_partner, j, zz, k)
         if what == BEGIN:
             mine = line(j, z, y) if both else piece(j, z, y, group)
             return [lambda: over_y(mine, j, yr.at[j]), lambda: inward(line(j, z, y), j, z, 1)]
@@ -530,7 +539,7 @@
         if what == ALONG:
             kept = pair(j, zz, group) if form == PAIRED else piece(j, zz, y, group)
             return [lambda: outward(kept, j, zz), lambda: over_x(pair(j, zz, group), j, xr.at[j, zz])]
-        return [lambda: to_partner(j, zz)]
+        return [lambda: to_partner(j, zz, p)]
 
     first_chunk = [sum(GROUPS[:g]) for g in range(len(GROUPS))]
 
@@ -623,16 +632,32 @@
 
     def project(g):
         at_chunk, wide = first_chunk[g], GROUPS[g] * width
-        blocks = []
-        for j in range(at_chunk, at_chunk + GROUPS[g]):
-            wait(wbuf.at[j, :, :, other_core], cr.at[j])
-            blocks.append(wbuf[j].reshape(work.features, width))
-        weights = blocks[0] if len(blocks) == 1 else jnp.concatenate(blocks, axis=1)
+        here = range(at_chunk, at_chunk + GROUPS[g])
+        each = work.features // depth
+
+        def block(layers, count_of, sems):
+            def ready():
+                for j in here:
+                    wait(wbuf.at[j, layers, :, other_core], sems.at[j])
+
+            def read():
+                parts = [wbuf[j, layers].reshape(count_of * each, width) for j in here]
+                return parts[0] if len(parts) == 1 else jnp.concatenate(parts, axis=1)
+
+            return ready, read
+
+        far = (1 - high) * (depth - 1)
+        ready, read = block(pl.ds(high, depth - 1), depth - 1, cr)
+        ready_far, read_far = block(pl.ds(far, 1), 1, cl)
+        blocks = [
+            (ready, pl.multiple_of(high * each, each), read),
+            (ready_far, pl.multiple_of(far * each, each), read_far),
+        ]
 
         def put(at_row, page):
             pbuf[g, at_row : at_row + PAGE, 0:wide] = page
 
-        work.project(weights, at_chunk < per_kind, put)
+        work.project(blocks, at_chunk < per_kind, put)
         pages_on_chip(g)
 
     sixteenth = tok_rows // 16
@@ -817,7 +842,7 @@
                 pbuf[j, at_row : at_row + PAGE, at : at + TILE] = page
 
             weights = wbuf[j, :, :, :, :, :, at : at + TILE].reshape(work.features, TILE)
-            work.project(weights, j < per_kind, put)
+            work.project([(lambda: None, 0, lambda: weights)], j < per_kind, put)
 
     def spot(j, region):
         rows = pl.ds(region * BLOCK, BLOCK)
@@ -912,7 +937,7 @@
     if in_line:
         slots = dma((groups, 2))
         scratch += [each, each, by_layer, by_layer, each, each, by_layer, each, each, by_layer, by_layer,
-                    each, each, by_region, by_region, slots, slots]
+                    each, each, each, by_region, by_region, slots, slots]
     else:
         by_line = dma((chunks, 2, depth))
         scratch += [each, dma((chunks, 2)), by_line, by_line, each, by_line, each, each,

time: 90.1 us -> 89.5 us (level)
  no operation moved by 1% of the time
where the time goes in v3:
time: 89.5 us; the launch traced here: 89.3 us
  Pallas kernels  87.8 us (98%)
  local copies, waits for them, and re-layouts  1.49 us (2%)
    pallas_call x1, Pallas kernels, on_device(): pl.pallas_call(functools.partial(line_kernel if in_line else loop_kernel,...  87.8 us

profile of v3, /device:TPU:1, one launch (start us, length us, event | category | flops | bytes accessed | tf_op | source)
XLA Modules:
  0.0 89.3 jit_solution(8982687297764627116)
XLA Ops:
  0.0 87.8 %shard_map.73 = bf16[2,640,1024]{2,1,0:T(8,128)(2,1)S(1)} custom-call(bf16[512,4096]{1,0:T(8,128)(2,1)} %tokens.1, bf16[32,128]{1,0:T(8,128)(2,1)} %bitcast.3, bf16[256,1024]{1,0:T(8,128)(2,1)} %w_key.1, bf16[256,1024]{1,0:T(8,128)(2,1)} %w_value.1, s32[2]{0:T(128)} %lengths.1, s32[32]{0:T(128)} %pages.1, f32[1,128]{1,0:T(1,128)} %constant.2.clone.freq), custom_call_target="tpu_custom_call" | custom-call | tf_op jit(solution)/shard_map/pallas_call | solution.py:945
  87.8 1.5 %copy.9 = bf16[2,40,16,1024]{3,2,1,0:T(8,128)(2,1)} copy(bf16[2,40,16,1024]{3,2,1,0:T(8,128)(2,1)S(1)} %bitcast.2) | data formatting | bytes 5242880
